TPU v7x, 16 devices: a whole 2x2x2 slice. The times are simulated.
16 devices in a mesh: dp: 2 (over z), tp: 8 (over y, x, core).
Axes of the slice: x: 2, y: 2, z: 2, core: 2. Of those that a mesh axis runs over, the one named last changes fastest.
Arguments:
- tok_hidden: bfloat16 [128, 3072], P('dp'), parts along dimension 0
- seq_lens: int32 [128], P('dp'), parts along dimension 0
- k_cache: bfloat16 [128, 512, 8, 128], P('dp', None, 'tp'), parts along dimension 0
- v_cache: bfloat16 [128, 512, 8, 128], P('dp', None, 'tp'), parts along dimension 0
- next_tok: int32 [128], P('dp'), parts along dimension 0
- g_attn: bfloat16 [3072], replicated
- w_q: bfloat16 [3072, 3072], P(None, 'tp')
- b_q: bfloat16 [3072], P('tp')
- w_k: bfloat16 [3072, 1024], P(None, 'tp')
- b_k: bfloat16 [1024], P('tp')
- w_v: bfloat16 [3072, 1024], P(None, 'tp')
- b_v: bfloat16 [1024], P('tp')
- w_o: bfloat16 [3072, 3072], P('tp')
- g_mlp: bfloat16 [3072], replicated
- w_gate: bfloat16 [3072, 8192], P(None, 'tp')
- w_up: bfloat16 [3072, 8192], P(None, 'tp')
- w_down: bfloat16 [8192, 3072], P('tp')
- g_final: bfloat16 [3072], replicated
- w_head: bfloat16 [128256, 3072], P('tp')
Outputs:
- output 1: bfloat16 [128, 3072], P('dp'), parts along dimension 0
- output 2: bfloat16 [128, 512, 8, 128], P('dp', None, 'tp'), parts along dimension 0
- output 3: bfloat16 [128, 512, 8, 128], P('dp', None, 'tp'), parts along dimension 0
- output 4: float32 [128], P('dp'), parts along dimension 0
- output 5: float32 [128], P('dp'), parts along dimension 0
There are 2 independent parts. A program takes and returns all parts, laid end to end along the dimension named above; an argument that names none is the same for every part.
All inputs are finite; a program needn't handle non-finite values.
Results may differ from a plain program's by a relative error of at most 0.0134478.
Values are sent between devices in bfloat16 or wider.
A program may use at most 1 GiB of HBM per device.

v0:
```python
import jax
import jax.numpy as jnp
from jax import lax
from jax.sharding import PartitionSpec as P

THETA = 1000000.0
EPS = 1e-6


def rms_norm(values, gain_vec):
    vals_f32 = values.astype(jnp.float32)
    inv_rms = lax.rsqrt(jnp.mean(vals_f32 * vals_f32, axis=-1, keepdims=True) + EPS)
    return (vals_f32 * inv_rms * gain_vec.astype(jnp.float32)).astype(jnp.bfloat16)


def rotary(values, positions):
    half_dim = values.shape[-1] // 2
    inv_freq = jnp.power(THETA, jnp.arange(half_dim, dtype=jnp.float32) * (-2.0 / values.shape[-1]))
    angles = positions.astype(jnp.float32)[:, None] * inv_freq[None, :]
    cos_part = jnp.cos(angles)[:, None, :]
    sin_part = jnp.sin(angles)[:, None, :]
    first_half = values[..., :half_dim]
    second_half = values[..., half_dim:]
    return jnp.concatenate([first_half * cos_part - second_half * sin_part, second_half * cos_part + first_half * sin_part], axis=-1)


def attention_block(tok_hidden, seq_lens, k_cache, v_cache, g_attn, w_q, b_q, w_k, b_k, w_v, b_v):
    num_rows = tok_hidden.shape[0]
    cache_len = k_cache.shape[1]
    slot_count = k_cache.shape[2]
    head_dim = k_cache.shape[3]
    head_count = w_q.shape[1] // head_dim
    group_size = head_count // slot_count
    normed = rms_norm(tok_hidden, g_attn)
    q_proj = jnp.dot(normed, w_q, preferred_element_type=jnp.float32) + b_q.astype(jnp.float32)
    k_proj = jnp.dot(normed, w_k, preferred_element_type=jnp.float32) + b_k.astype(jnp.float32)
    v_proj = jnp.dot(normed, w_v, preferred_element_type=jnp.float32) + b_v.astype(jnp.float32)
    q_rot = rotary(q_proj.reshape(num_rows, head_count, head_dim), seq_lens).astype(jnp.bfloat16)
    k_new = rotary(k_proj.reshape(num_rows, slot_count, head_dim), seq_lens).astype(jnp.bfloat16)
    v_new = v_proj.reshape(num_rows, slot_count, head_dim).astype(jnp.bfloat16)
    slot_ids = lax.broadcasted_iota(jnp.int32, (1, cache_len, 1, 1), 1)
    write_mask = slot_ids == seq_lens[:, None, None, None]
    k_all = jnp.where(write_mask, k_new[:, None], k_cache)
    v_all = jnp.where(write_mask, v_new[:, None], v_cache)
    q_grp = q_rot.reshape(num_rows, slot_count, group_size, head_dim)
    scores = jnp.einsum('bkgd,blkd->bkgl', q_grp, k_all, preferred_element_type=jnp.float32) * (head_dim ** -0.5)
    score_ids = lax.broadcasted_iota(jnp.int32, (1, 1, 1, cache_len), 3)
    scores = jnp.where(score_ids <= seq_lens[:, None, None, None], scores, -jnp.inf)
    row_max = jnp.max(scores, axis=-1, keepdims=True)
    exp_scores = jnp.exp(scores - row_max)
    attn_probs = (exp_scores / jnp.sum(exp_scores, axis=-1, keepdims=True)).astype(jnp.bfloat16)
    attn_vals = jnp.einsum('bkgl,blkd->bkgd', attn_probs, v_all, preferred_element_type=jnp.float32)
    attn_out = attn_vals.astype(jnp.bfloat16).reshape(num_rows, head_count * head_dim)
    return attn_out, k_all, v_all


def local_step(tok_hidden, seq_lens, k_cache, v_cache, next_tok, g_attn, w_q, b_q, w_k, b_k, w_v, b_v, w_o, g_mlp, w_gate, w_up, w_down, g_final, w_head):
    attn_out, k_all, v_all = attention_block(tok_hidden, seq_lens, k_cache, v_cache, g_attn, w_q, b_q, w_k, b_k, w_v, b_v)
    attn_part = jnp.dot(attn_out, w_o, preferred_element_type=jnp.float32).astype(jnp.bfloat16)
    attn_sum = lax.psum(attn_part, 'tp')
    residual = (tok_hidden.astype(jnp.float32) + attn_sum.astype(jnp.float32)).astype(jnp.bfloat16)
    mlp_in = rms_norm(residual, g_mlp)
    gate_proj = jnp.dot(mlp_in, w_gate, preferred_element_type=jnp.float32)
    up_proj = jnp.dot(mlp_in, w_up, preferred_element_type=jnp.float32)
    hidden = (jax.nn.silu(gate_proj) * up_proj).astype(jnp.bfloat16)
    down_part = jnp.dot(hidden, w_down, preferred_element_type=jnp.float32).astype(jnp.bfloat16)
    down_sum = lax.psum(down_part, 'tp')
    y_out = (residual.astype(jnp.float32) + down_sum.astype(jnp.float32)).astype(jnp.bfloat16)
    final_norm = rms_norm(y_out, g_final)
    logits = lax.dot_general(final_norm, w_head, (((1,), (1,)), ((), ())), preferred_element_type=jnp.float32)
    vocab_loc = w_head.shape[0]
    vocab_ids = lax.broadcasted_iota(jnp.int32, (1, vocab_loc), 1)
    local_tok = next_tok - lax.axis_index('tp') * vocab_loc
    local_max = jnp.max(logits, axis=1)
    local_sum = jnp.sum(jnp.exp(logits - local_max[:, None]), axis=1)
    local_target = jnp.sum(jnp.where(vocab_ids == local_tok[:, None], logits, 0.0), axis=1)
    all_stats = lax.all_gather(jnp.stack([local_max, local_sum, local_target]), 'tp')
    glob_max = jnp.max(all_stats[:, 0], axis=0)
    exp_total = jnp.sum(all_stats[:, 1] * jnp.exp(all_stats[:, 0] - glob_max[None, :]), axis=0)
    norm_lse = glob_max + jnp.log(exp_total)
    tok_logp = jnp.sum(all_stats[:, 2], axis=0) - norm_lse
    return y_out, k_all, v_all, tok_logp, norm_lse


def solution(mesh):
    row_spec = P('dp', None)
    vec_spec = P('dp')
    cache_spec = P('dp', None, 'tp', None)
    col_spec = P(None, 'tp')
    part_spec = P('tp')
    whole_spec = P(None)
    in_specs = (row_spec, vec_spec, cache_spec, cache_spec, vec_spec, whole_spec, col_spec, part_spec, col_spec, part_spec, col_spec, part_spec, P('tp', None), whole_spec, col_spec, col_spec, P('tp', None), whole_spec, P('tp', None))
    out_specs = (row_spec, cache_spec, cache_spec, vec_spec, vec_spec)
    return jax.shard_map(local_step, mesh=mesh, in_specs=in_specs, out_specs=out_specs, check_vma=False)
```

profile of v0, /device:TPU:0, one launch (start us, length us, event | category | flops | bytes accessed | tf_op | source)
XLA Modules:
  0.0 212.7 jit_solution(15201512856477094611)
XLA Ops:
  7.2 0.8 convert_element_type.89
  8.1 0.8 iota_compare_fusion.2
  8.8 0.7 convert_element_type.86
  9.5 1.2 fusion.22
  10.7 0.7 convert_element_type.90
  11.6 1.6 fusion.14
  13.3 0.7 convert_element_type.92
  14.0 0.7 convert_element_type.88
  14.7 2.4 %convolution_add_fusion = f32[64,384]{1,0:T(8,128)S(1)} fusion(bf16[3072,384]{1,0:T(8,128)(2,1)} %param.25, f32[384]{0:T(512)S(1)} %convert_element_type.88, bf16[64,3072]{1,0:T(8,128)(2,1)} %param.19, f32[3072]{0:T(1024)S(1)} %convert_element_type.86, f32[64]{0:T(128)S(1)} %add_rsqrt_fusion.2), kind=kOutput, calls=%fused_computation.24 | convolution fusion | flops 151805952 | bytes 2864896 | tf_op jit(solution)/shard_map/dot_general | solution.py:35
  17.2 1.6 fusion.18
  18.9 11.9 %broadcast_select_fusion.1 = (bf16[64,512,1,128]{3,1,2,0:T(8,128)(2,1)}, bf16[64,512,1,128]{3,1,2,0:T(8,128)(2,1)}) fusion(bf16[64,512,1,128]{3,1,2,0:T(8,128)(2,1)} %param.21, pred[64,512]{1,0:T(8,128)(4,1)S(1)} %get-tuple-element.26, bf16[64,128]{1,0:T(8,128)(2,1)S(1)} %pad_maximum_fusion, bf16[64,512,1,128]{3,1,2,0:T(8,128)(2,1)} %param.22, ...), kind=kLoop, calls=%fused_computation.6 | loop fusion | flops 8388608 | bytes 33619968 | tf_op jit(solution)/shard_map/jit(_where)/select_n | solution.py:43
  30.8 5.9 %fusion.68 = (f32[64,3]{1,0:T(8,128)S(1)}, f32[64,3,512]{2,1,0:T(4,128)S(1)}) fusion(bf16[64,512,1,128]{3,1,2,0:T(8,128)(2,1)} %get-tuple-element.19, pred[64,512]{1,0:T(8,128)(4,1)S(1)} %get-tuple-element.25, bf16[64,3,64]{2,1,0:T(4,128)(2,1)S(1)} %get-tuple-element.16, bf16[64,3,64]{2,1,0:T(4,128)(2,1)S(1)} %get-tuple-element.15), kind=kOutput, calls=%fused_computation.92 | convolution fusion | flops 25657856 | bytes 8864512 | tf_op jit(solution)/shard_map/sub | solution.py:50
  36.6 4.7 %fusion.11 = bf16[64,3,128]{2,1,0:T(4,128)(2,1)S(1)} fusion(bf16[64,512,1,128]{3,1,2,0:T(8,128)(2,1)} %get-tuple-element.20, f32[64,3,512]{2,1,0:T(4,128)S(1)} %get-tuple-element.28, f32[64,3]{1,0:T(8,128)S(1)} %get-tuple-element.27), kind=kOutput, calls=%fused_computation.23 | convolution fusion | flops 25387008 | bytes 8831744 | tf_op jit(solution)/shard_map/bkgl,blkd->bkgd/dot_general | solution.py:52
  41.3 1.3 convolution_convert_fusion.1
  42.8 49.5 %all-reduce.3.cloned.1.call-done = bf16[64,3072]{1,0:T(8,128)(2,1)} async-done(((bf16[64,3072]{1,0:T(8,128)(2,1)}), bf16[64,3072]{1,0:T(8,128)(2,1)}) %all-reduce.3.cloned.1.call-update) | async-done | bytes 393232 | tf_op jit(solution)/shard_map/psum | solution.py:60
  92.2 1.2 fusion.26
  93.5 4.0 %fusion.43 = f32[64,1024]{1,0:T(8,128)S(1)} fusion(bf16[3072,1024]{1,0:T(8,128)(2,1)} %param.33, bf16[64,3072]{1,0:T(8,128)(2,1)S(1)} %get-tuple-element.14, f32[3072]{0:T(1024)S(1)} %convert_element_type.99, f32[64]{0:T(128)S(1)} %add_rsqrt_fusion.1), kind=kOutput, calls=%fused_computation.58 | convolution fusion | flops 403439616 | bytes 6959360 | tf_op jit(solution)/shard_map/dot_general | solution.py:63
  97.6 7.7 %convolution_convert_fusion = bf16[64,3072]{1,0:T(8,128)(2,1)} fusion(bf16[1024,3072]{1,0:T(8,128)(2,1)} %param.35, bf16[3072,1024]{1,0:T(8,128)(2,1)} %param.34, f32[64,1024]{1,0:T(8,128)S(1)} %fusion.43, bf16[64,3072]{1,0:T(8,128)(2,1)S(1)} %get-tuple-element.14, f32[3072]{0:T(1024)S(1)} %convert_element_type.99, f32[64]{0:T(128)S(1)} %add_rsqrt_fusion.1), kind=kOutput, calls=%fused_computation.10 | convolution fusion | flops 806682624 | bytes 13644032 | tf_op jit(solution)/shard_map/dot_general | solution.py:66
  105.3 46.0 %all-reduce.5.cloned.1.call-done = bf16[64,3072]{1,0:T(8,128)(2,1)} async-done(((bf16[64,3072]{1,0:T(8,128)(2,1)}), bf16[64,3072]{1,0:T(8,128)(2,1)}) %all-reduce.5.cloned.1.call-update) | async-done | bytes 393232 | tf_op jit(solution)/shard_map/psum | solution.py:67
  151.3 1.2 fusion.19
  152.6 41.3 %fusion.69 = (f32[64]{0:T(128)S(1)}, f32[64,16032]{1,0:T(8,128)}) fusion(bf16[16032,3072]{1,0:T(8,128)(2,1)} %param.37, bf16[64,3072]{1,0:T(8,128)(2,1)S(1)} %get-tuple-element.12, f32[3072]{0:T(1024)S(1)} %convert_element_type.106, f32[64]{0:T(128)S(1)} %add_rsqrt_fusion), kind=kOutput, calls=%fused_computation.93 | convolution fusion | flops 6305851392 | bytes 103010816 | tf_op jit(solution)/shard_map/dot_general | solution.py:70
  193.9 3.3 %exponential_reduce_fusion = (f32[64]{0:T(128)S(1)}, f32[64]{0:T(128)S(1)}) fusion(f32[64,16032]{1,0:T(8,128)} %get-tuple-element.30, f32[64]{0:T(128)S(1)} %get-tuple-element.29, s32[64]{0:T(128)S(1)} %broadcast_subtract_fusion), kind=kLoop, calls=%fused_computation.9 | loop fusion | flops 5130112 | bytes 4105216 | tf_op jit(solution)/shard_map/reduce_sum | solution.py:75
  197.2 8.1 %all-gather.1 = f32[8,3,64]{2,1,0:T(4,128)S(1)} all-gather(f32[1,3,64]{2,1,0:T(4,128)S(1)} %maximum_bitcast_fusion), channel_id=2, replica_groups=mesh['dp'=2,'tp'=8] {'tp'}, dimensions={0}, use_global_device_ids=true | all-gather | bytes 6912 | tf_op jit(solution)/shard_map/all_gather | solution.py:77
  205.4 0.5 fusion.65
  (33 shorter events, 0.9 us)
Async XLA Ops:
  7.2 34.2 %copy-start = (bf16[384,3072]{1,0:T(8,128)(2,1)S(1)}, bf16[384,3072]{1,0:T(8,128)(2,1)}, u32[]{:S(2)}) copy-start(bf16[384,3072]{1,0:T(8,128)(2,1)} %param.31) | copy-start | bytes 7077892
  7.2 85.1 %all-reduce.3.cloned.1.call-start = ((), (), s32[]{:S(2)}) async-start(), calls=%async_computation | async-start | bytes 786432 | tf_op jit(solution)/shard_map/psum | solution.py:60
  36.6 6.1 %copy-start.4 = (bf16[3072]{0:T(1024)(128)(2,1)S(1)}, bf16[3072]{0:T(1024)(128)(2,1)}, u32[]{:S(2)}) copy-start(bf16[3072]{0:T(1024)(128)(2,1)} %param.32) | copy-start | bytes 18436
  36.6 6.1 %copy-start.5 = (bf16[3072]{0:T(1024)(128)(2,1)S(1)}, bf16[3072]{0:T(1024)(128)(2,1)}, u32[]{:S(2)}) copy-start(bf16[3072]{0:T(1024)(128)(2,1)} %param.36) | copy-start | bytes 18436
  36.6 55.6 %copy-start.2 = (bf16[64,3072]{1,0:T(8,128)(2,1)S(1)}, bf16[64,3072]{1,0:T(8,128)(2,1)}, u32[]{:S(2)}) copy-start(bf16[64,3072]{1,0:T(8,128)(2,1)} %param.19) | copy-start | bytes 1179652
  42.7 108.7 %all-reduce.5.cloned.1.call-start = ((), (), s32[]{:S(2)}) async-start(), calls=%async_computation.1 | async-start | bytes 786432 | tf_op jit(solution)/shard_map/psum | solution.py:67
  97.5 7.8 %copy-start.6 = (s32[64]{0:T(128)S(1)}, s32[64]{0:T(128)}, u32[]{:S(2)}) copy-start(s32[64]{0:T(128)} %param.23) | copy-start | bytes 772
  152.6 41.3 %copy-start.3 = (bf16[64,3072]{1,0:T(8,128)(2,1)}, bf16[64,3072]{1,0:T(8,128)(2,1)S(1)}, u32[]{:S(2)}) copy-start(bf16[64,3072]{1,0:T(8,128)(2,1)S(1)} %get-tuple-element.12) | copy-start | bytes 1179652
  152.6 53.3 %copy-start.1 = (bf16[384,3072]{1,0:T(8,128)(2,1)S(1)}, bf16[384,3072]{1,0:T(8,128)(2,1)}, u32[]{:S(2)}) copy-start(bf16[384,3072]{1,0:T(8,128)(2,1)} %param.31) | copy-start | bytes 7077892
Sparse Core Ops, SparseCore 0:
  42.8 49.4 all-reduce.2
  105.4 45.8 all-reduce.4
where the time goes:
time: 213 us
  waiting for transfers between devices  95.5 us (45%)
  matrix products  70.4 us (33%)
  other arithmetic  24.3 us (11%)
  between operations  14.2 us (7%)
  blocking collectives  8.07 us (4%)
    psum x1, waiting for transfers between devices, local_step(): attn_sum = lax.psum(attn_part, 'tp')  49.5 us
    psum x1, waiting for transfers between devices, local_step(): down_sum = lax.psum(down_part, 'tp')  46 us
    dot_general x1, matrix products, local_step(): lax.dot_general(final_norm, w_head, (((1,), (1,)), ((), ())), preferred_e...  41.3 us
    select_n x1, other arithmetic, attention_block(): k_all = jnp.where(write_mask, k_new[:, None], k_cache)  11.9 us
    all_gather x1, blocking collectives, local_step(): lax.all_gather(jnp.stack([local_max, local_sum, local_target]), 'tp')  8.07 us
    dot_general x1, matrix products, local_step(): jnp.dot(hidden, w_down, preferred_element_type=jnp.float32)  7.72 us
    sub x1, matrix products, attention_block(): exp_scores = jnp.exp(scores - row_max)  5.87 us
    dot_general x1, matrix products, attention_block(): jnp.einsum('bkgl,blkd->bkgd', attn_probs, v_all, preferred_element_type=j...  4.68 us
  transfers between devices with their start and end apart: 2, of which 2 were waited for; matrix products, arithmetic and copies ran while one was open for 0% of the time, Pallas kernels for 0%

commit v1 on v0

v1 whole, which is shorter than its diff:
```python
import functools

import jax
import jax.numpy as jnp
from jax import lax
from jax.experimental import pallas as pl
from jax.experimental.pallas import tpu as pltpu
from jax.sharding import PartitionSpec as P

THETA = 1000000.0
EPS = 1e-6
MESH = pl.DeviceIdType.MESH
GROUP_ROWS = 8
HEAD_ROWS = 1024
HEAD_SLOTS = 5
FLIPS = ((1, 1, 0), (1, 1, 1), (0, 1, 0), (1, 0, 0), (0, 1, 1), (1, 0, 1), (0, 0, 1))
NT = (((1,), (1,)), ((), ()))


def rms_scaled(vals_f32, gain_f32):
    inv_rms = lax.rsqrt(jnp.mean(vals_f32 * vals_f32, axis=-1, keepdims=True) + EPS)
    return (vals_f32 * inv_rms * gain_f32).astype(jnp.bfloat16)


def attention_kernel(len_ref, x_ref, g_ref, bq_ref, bk_ref, bv_ref, cos_ref, sin_ref, wq_hbm, wk_hbm, wv_hbm, kc_hbm, vc_hbm,
                     attn_ref, ko_hbm, vo_hbm,
                     wq, wk, wv, kbuf, vbuf, normed, q_scr, kn_scr, vn_scr, o_scr, w_sem, in_sem, out_sem):
    rows, cache_len, head_dim = kbuf.shape
    heads = wq.shape[1] // head_dim
    groups = rows // GROUP_ROWS
    weight_copies = [pltpu.make_async_copy(src, dst, w_sem.at[i]) for i, (src, dst) in enumerate(((wq_hbm, wq), (wk_hbm, wk), (wv_hbm, wv)))]
    for copy in weight_copies:
        copy.start()

    def loads(g):
        part = pl.ds(g * GROUP_ROWS, GROUP_ROWS)
        return (pltpu.make_async_copy(kc_hbm.at[part], kbuf.at[part], in_sem.at[0, g]),
                pltpu.make_async_copy(vc_hbm.at[part], vbuf.at[part], in_sem.at[1, g]))

    def stores(g):
        part = pl.ds(g * GROUP_ROWS, GROUP_ROWS)
        return (pltpu.make_async_copy(kbuf.at[part], ko_hbm.at[part], out_sem.at[0, g]),
                pltpu.make_async_copy(vbuf.at[part], vo_hbm.at[part], out_sem.at[1, g]))

    for g in range(groups):
        for copy in loads(g):
            copy.start()

    normed[...] = rms_scaled(x_ref[...].astype(jnp.float32), g_ref[...].astype(jnp.float32))
    q_scr[...] = jnp.zeros_like(q_scr)
    cos_part = cos_ref[...]
    sin_part = sin_ref[...]

    def rotate(vals):
        return vals * cos_part + pltpu.roll(vals, head_dim // 2, 1) * sin_part

    for copy in weight_copies:
        copy.wait()
    q_proj = jnp.dot(normed[...], wq[...], preferred_element_type=jnp.float32) + bq_ref[...].astype(jnp.float32)
    for h in range(heads):
        q_scr[pl.ds(h, rows, stride=8), :] = rotate(q_proj[:, h * head_dim:(h + 1) * head_dim])
    k_proj = jnp.dot(normed[...], wk[...], preferred_element_type=jnp.float32) + bk_ref[...].astype(jnp.float32)
    kn_scr[...] = rotate(k_proj)
    vn_scr[...] = jnp.dot(normed[...], wv[...], preferred_element_type=jnp.float32) + bv_ref[...].astype(jnp.float32)

    tile_ids = lax.broadcasted_iota(jnp.int32, (16, head_dim), 0)
    slot_ids = lax.broadcasted_iota(jnp.int32, (8, cache_len), 1)

    def patch(buf, new_ref, row, length):
        base = pl.multiple_of((length // 16) * 16, 16)
        tile = buf[row, pl.ds(base, 16), :].astype(jnp.float32)
        new = jnp.broadcast_to(new_ref[pl.ds(row, 1), :], tile.shape)
        buf[row, pl.ds(base, 16), :] = jnp.where(tile_ids == length - base, new, tile).astype(jnp.bfloat16)

    @pl.loop(0, groups)
    def group(g):
        for copy in loads(g):
            copy.wait()
        for j in range(GROUP_ROWS):
            row = g * GROUP_ROWS + j
            length = len_ref[row]
            patch(kbuf, kn_scr, row, length)
            patch(vbuf, vn_scr, row, length)
        probs = []
        for j in range(GROUP_ROWS):
            row = g * GROUP_ROWS + j
            q_row = q_scr[pl.ds(pl.multiple_of(row * 8, 8), 8), :].astype(jnp.bfloat16)
            scores = lax.dot_general(q_row, kbuf[row], NT, preferred_element_type=jnp.float32) * (head_dim ** -0.5)
            scores = jnp.where(slot_ids <= len_ref[row], scores, -jnp.inf)
            exp_scores = jnp.exp(scores - jnp.max(scores, axis=-1, keepdims=True))
            probs.append((exp_scores / jnp.sum(exp_scores, axis=-1, keepdims=True)).astype(jnp.bfloat16))
        for j in range(GROUP_ROWS):
            row = g * GROUP_ROWS + j
            o_scr[pl.ds(pl.multiple_of(row * 8, 8), 8), :] = jnp.dot(probs[j], vbuf[row], preferred_element_type=jnp.float32)
        for copy in stores(g):
            copy.start()

    for h in range(heads):
        attn_ref[:, h * head_dim:(h + 1) * head_dim] = o_scr[pl.ds(h, rows, stride=8), :].astype(jnp.bfloat16)
    for g in range(groups):
        for copy in stores(g):
            copy.wait()


def tail_kernel(attn_ref, x_ref, gm_ref, gf_ref, tok_ref, wo_hbm, wg_hbm, wu_hbm, wd_hbm, wh_hbm,
                y_ref, logp_ref, lse_ref,
                wo, wg, wu, wd, ring, send1, recv1, send2, recv2, a_full, normed, gate_act, stat_send, stat_recv,
                w_sem, ring_sem, send_sem, recv_sem):
    rows, width = x_ref.shape
    part = width // 8
    vocab = wh_hbm.shape[0]
    ff = wg.shape[1]
    chunks = pl.cdiv(vocab, HEAD_ROWS)
    me = lax.axis_index('tp')
    my_y, my_x, my_c = me // 4, (me // 2) % 2, me % 2

    def peer(flip):
        fy, fx, fc = flip
        pos_y = 1 - my_y if fy else my_y
        pos_x = 1 - my_x if fx else my_x
        pos_c = 1 - my_c if fc else my_c
        return pos_y * 4 + pos_x * 2 + pos_c

    def columns(who):
        return pl.ds(pl.multiple_of(who * part, 128), part)

    peers = [peer(flip) for flip in FLIPS]
    wo_copy = pltpu.make_async_copy(wo_hbm, wo, w_sem.at[0])
    wo_copy.start()
    barrier = pltpu.get_barrier_semaphore()
    for who in peers:
        pl.semaphore_signal(barrier, inc=1, device_id={'tp': who}, device_id_type=MESH)

    def head_copy(i):
        start = pl.multiple_of(jnp.minimum(i * HEAD_ROWS, vocab - HEAD_ROWS), 16)
        return pltpu.make_async_copy(wh_hbm.at[pl.ds(start, HEAD_ROWS)], ring.at[i % HEAD_SLOTS], ring_sem.at[i % HEAD_SLOTS])

    mlp_copies = [pltpu.make_async_copy(src, dst, w_sem.at[i + 1]) for i, (src, dst) in enumerate(((wg_hbm, wg), (wu_hbm, wu), (wd_hbm, wd)))]
    wo_copy.wait()
    for copy in mlp_copies:
        copy.start()
    for i in range(HEAD_SLOTS):
        head_copy(i).start()
    pl.semaphore_wait(barrier, len(FLIPS))

    def scatter_sum(stage, lhs, weight, send, recv, base):
        copies = []
        for k, who in enumerate(peers):
            send[k] = jnp.dot(lhs, weight[:, columns(who)], preferred_element_type=jnp.float32).astype(jnp.bfloat16)
            copy = pltpu.make_async_remote_copy(
                src_ref=send.at[k], dst_ref=recv.at[k], send_sem=send_sem.at[stage, k], recv_sem=recv_sem.at[stage, k],
                device_id={'tp': who}, device_id_type=MESH)
            copy.start()
            copies.append(copy)
        total = jnp.dot(lhs, weight[:, columns(me)], preferred_element_type=jnp.float32)
        for k in reversed(range(len(FLIPS))):
            copies[k].wait_recv()
            total = total + recv[k].astype(jnp.float32)
        return (base + total).astype(jnp.bfloat16), copies

    def gather(stage, full):
        copies = []
        for k, who in enumerate(peers):
            copy = pltpu.make_async_remote_copy(
                src_ref=full.at[:, columns(me)], dst_ref=full.at[:, columns(me)],
                send_sem=send_sem.at[stage, k], recv_sem=recv_sem.at[stage, k],
                device_id={'tp': who}, device_id_type=MESH)
            copy.start()
            copies.append(copy)
        for k, who in enumerate(peers):
            pltpu.make_async_remote_copy(
                src_ref=full.at[:, columns(who)], dst_ref=full.at[:, columns(who)],
                send_sem=send_sem.at[stage, k], recv_sem=recv_sem.at[stage, k],
                device_id={'tp': who}, device_id_type=MESH).wait_recv()
        return copies

    pending = []
    a_part, copies = scatter_sum(0, attn_ref[...], wo, send1, recv1, x_ref[:, columns(me)].astype(jnp.float32))
    pending += copies
    a_full[:, columns(me)] = a_part
    pending += gather(1, a_full)
    normed[...] = rms_scaled(a_full[...].astype(jnp.float32), gm_ref[...].astype(jnp.float32))

    mlp_copies[0].wait()
    mlp_copies[1].wait()

    @pl.loop(0, ff // 256)
    def mlp(i):
        cols = pl.ds(pl.multiple_of(i * 256, 256), 256)
        gate = jnp.dot(normed[...], wg[:, cols], preferred_element_type=jnp.float32)
        up = jnp.dot(normed[...], wu[:, cols], preferred_element_type=jnp.float32)
        gate_act[:, cols] = (jax.nn.silu(gate) * up).astype(jnp.bfloat16)

    mlp_copies[2].wait()
    y_part, copies = scatter_sum(2, gate_act[...], wd, send2, recv2, a_full[:, columns(me)].astype(jnp.float32))
    pending += copies
    y_ref[:, columns(me)] = y_part
    pending += gather(3, y_ref)
    normed[...] = rms_scaled(y_ref[...].astype(jnp.float32), gf_ref[...].astype(jnp.float32))

    lane_ids = lax.broadcasted_iota(jnp.int32, (rows, 128), 1)
    local_tok = tok_ref[...] - me * vocab

    def head_step(i, carry):
        run_max, run_sum, run_tgt = carry
        head_copy(i).wait()
        logits = lax.dot_general(normed[...], ring[i % HEAD_SLOTS], NT, preferred_element_type=jnp.float32)

        @pl.when(i + HEAD_SLOTS < chunks)
        def _():
            head_copy(i + HEAD_SLOTS).start()

        start = jnp.minimum(i * HEAD_ROWS, vocab - HEAD_ROWS)
        slabs = []
        new_max = run_max
        for s in range(HEAD_ROWS // 128):
            ids = lane_ids + (start + s * 128)
            slab = jnp.where(ids >= i * HEAD_ROWS, logits[:, s * 128:(s + 1) * 128], -jnp.inf)
            run_tgt = run_tgt + jnp.where((ids == local_tok) & (ids >= i * HEAD_ROWS), slab, 0.0)
            new_max = jnp.maximum(new_max, slab)
            slabs.append(slab)
        run_sum = run_sum * jnp.exp(run_max - new_max)
        for slab in slabs:
            run_sum = run_sum + jnp.exp(slab - new_max)
        return new_max, run_sum, run_tgt

    zeros = jnp.zeros((rows, 128), jnp.float32)
    run_max, run_sum, run_tgt = lax.fori_loop(0, chunks, head_step, (jnp.full((rows, 128), -jnp.inf, jnp.float32), zeros, zeros))
    loc_max = jnp.max(run_max, axis=-1, keepdims=True)
    loc_sum = jnp.sum(run_sum * jnp.exp(run_max - loc_max), axis=-1, keepdims=True)
    loc_tgt = jnp.sum(run_tgt, axis=-1, keepdims=True)
    packed = jnp.where(lane_ids == 0, loc_max, jnp.where(lane_ids == 1, loc_sum, loc_tgt))
    packed = jnp.concatenate([packed, jnp.zeros((128 - rows, 128), jnp.float32)], axis=0)
    own = jnp.transpose(packed)[:8]
    stat_send[...] = own
    copies = []
    for k, who in enumerate(peers):
        copy = pltpu.make_async_remote_copy(
            src_ref=stat_send, dst_ref=stat_recv.at[k], send_sem=send_sem.at[4, k], recv_sem=recv_sem.at[4, k],
            device_id={'tp': who}, device_id_type=MESH)
        copy.start()
        copies.append(copy)
    stats = [own]
    for k in reversed(range(len(FLIPS))):
        copies[k].wait_recv()
        stats.append(stat_recv[k])
    pending += copies
    glob_max = functools.reduce(jnp.maximum, [s[0:1] for s in stats])
    exp_total = functools.reduce(jnp.add, [s[1:2] * jnp.exp(s[0:1] - glob_max) for s in stats])
    lse = glob_max + jnp.log(exp_total)
    target = functools.reduce(jnp.add, [s[2:3] for s in stats])
    lse_ref[...] = lse[:, :rows]
    logp_ref[...] = (target - lse)[:, :rows]
    for copy in pending:
        copy.wait_send()


def local_step(tok_hidden, seq_lens, k_cache, v_cache, next_tok, g_attn, w_q, b_q, w_k, b_k, w_v, b_v, w_o, g_mlp, w_gate, w_up, w_down, g_final, w_head):
    rows, width = tok_hidden.shape
    cache_shape = k_cache.shape
    cache_len, head_dim = cache_shape[1], cache_shape[3]
    bf16, f32 = jnp.bfloat16, jnp.float32
    half_dim = head_dim // 2
    inv_freq = jnp.power(THETA, jnp.arange(half_dim, dtype=f32) * (-2.0 / head_dim))
    angles = seq_lens.astype(f32)[:, None] * inv_freq[None, :]
    cos_half, sin_half = jnp.cos(angles), jnp.sin(angles)
    cos_part = jnp.concatenate([cos_half, cos_half], axis=-1)
    sin_part = jnp.concatenate([-sin_half, sin_half], axis=-1)
    flat = (rows, cache_len, head_dim)
    vmem = pl.BlockSpec(memory_space=pltpu.VMEM)
    smem = pl.BlockSpec(memory_space=pltpu.SMEM)
    hbm = pl.BlockSpec(memory_space=pl.ANY)
    groups = rows // GROUP_ROWS
    attn_out, k_all, v_all = pl.pallas_call(
        attention_kernel,
        out_shape=(jax.ShapeDtypeStruct((rows, w_q.shape[1]), bf16), jax.ShapeDtypeStruct(flat, bf16), jax.ShapeDtypeStruct(flat, bf16)),
        in_specs=[smem] + [vmem] * 7 + [hbm] * 5,
        out_specs=(vmem, hbm, hbm),
        scratch_shapes=[
            pltpu.VMEM(w_q.shape, bf16), pltpu.VMEM(w_k.shape, bf16), pltpu.VMEM(w_v.shape, bf16),
            pltpu.VMEM(flat, bf16), pltpu.VMEM(flat, bf16), pltpu.VMEM((rows, width), bf16),
            pltpu.VMEM((rows * 8, head_dim), f32), pltpu.VMEM((rows, head_dim), f32), pltpu.VMEM((rows, head_dim), f32),
            pltpu.VMEM((rows * 8, head_dim), f32),
            pltpu.SemaphoreType.DMA((3,)), pltpu.SemaphoreType.DMA((2, groups)), pltpu.SemaphoreType.DMA((2, groups)),
        ],
        compiler_params=pltpu.CompilerParams(vmem_limit_bytes=40 * 1024 * 1024),
        name='attention',
    )(seq_lens, tok_hidden, g_attn[None], b_q[None], b_k[None], b_v[None], cos_part, sin_part, w_q, w_k, w_v, k_cache.reshape(flat), v_cache.reshape(flat))

    part = width // 8
    peers = len(FLIPS)
    y_out, tok_logp, norm_lse = pl.pallas_call(
        tail_kernel,
        out_shape=(jax.ShapeDtypeStruct((rows, width), bf16), jax.ShapeDtypeStruct((1, rows), f32), jax.ShapeDtypeStruct((1, rows), f32)),
        in_specs=[vmem] * 5 + [hbm] * 5,
        out_specs=(vmem, vmem, vmem),
        scratch_shapes=[
            pltpu.VMEM(w_o.shape, bf16), pltpu.VMEM(w_gate.shape, bf16), pltpu.VMEM(w_up.shape, bf16), pltpu.VMEM(w_down.shape, bf16),
            pltpu.VMEM((HEAD_SLOTS, HEAD_ROWS, width), bf16),
            pltpu.VMEM((peers, rows, part), bf16), pltpu.VMEM((peers, rows, part), bf16),
            pltpu.VMEM((peers, rows, part), bf16), pltpu.VMEM((peers, rows, part), bf16),
            pltpu.VMEM((rows, width), bf16), pltpu.VMEM((rows, width), bf16), pltpu.VMEM((rows, w_gate.shape[1]), bf16),
            pltpu.VMEM((8, 128), f32), pltpu.VMEM((peers, 8, 128), f32),
            pltpu.SemaphoreType.DMA((4,)), pltpu.SemaphoreType.DMA((HEAD_SLOTS,)),
            pltpu.SemaphoreType.DMA((5, peers)), pltpu.SemaphoreType.DMA((5, peers)),
        ],
        compiler_params=pltpu.CompilerParams(vmem_limit_bytes=62 * 1024 * 1024, collective_id=0, has_side_effects=True),
        name='tail',
    )(attn_out, tok_hidden, g_mlp[None], g_final[None], next_tok[:, None], w_o, w_gate, w_up, w_down, w_head)
    return y_out, k_all.reshape(cache_shape), v_all.reshape(cache_shape), tok_logp.reshape(rows), norm_lse.reshape(rows)


def solution(mesh):
    row_spec = P('dp', None)
    vec_spec = P('dp')
    cache_spec = P('dp', None, 'tp', None)
    col_spec = P(None, 'tp')
    part_spec = P('tp')
    whole_spec = P(None)
    in_specs = (row_spec, vec_spec, cache_spec, cache_spec, vec_spec, whole_spec, col_spec, part_spec, col_spec, part_spec, col_spec, part_spec, P('tp', None), whole_spec, col_spec, col_spec, P('tp', None), whole_spec, P('tp', None))
    out_specs = (row_spec, cache_spec, cache_spec, vec_spec, vec_spec)
    return jax.shard_map(local_step, mesh=mesh, in_specs=in_specs, out_specs=out_specs, check_vma=False)
```

time: 213 us -> 103 us (0.48)
  waiting for transfers between devices: 95.5 us -> 0 us
  Pallas kernels: 0 us -> 80.5 us
  matrix products: 70.4 us -> 0 us
  other arithmetic: 24.3 us -> 0.95 us
  local copies, waits for them, and re-layouts: 0.08 us -> 20.3 us
  between operations: 14.2 us -> 0.69 us
  blocking collectives: 8.07 us -> 0 us
    psum x2 -> x0, waiting for transfers between devices: 95.5 us -> none  [the longest x1 49.5 us: local_step(): attn_sum = lax.psum(attn_part, 'tp')]
    pallas_call x0 -> x2, Pallas kernels: none -> 80.5 us  [the longest x1 71.2 us: local_step(): pl.pallas_call(tail_kernel, out_shape=(jax.ShapeDtypeStruct((rows, width)...]
    dot_general x8 -> x0, matrix products: 64.5 us -> none  [the longest x1 41.3 us: local_step(): lax.dot_general(final_norm, w_head, (((1,), (1,)), ((), ())), preferred_e...]
    unnamed x14 -> x21, local copies, waits for them, and re-layouts: 0.04 us -> 15 us
    select_n x1 -> x0, other arithmetic: 11.9 us -> none  [attention_block(): k_all = jnp.where(write_mask, k_new[:, None], k_cache)]
    all_gather x1 -> x0, blocking collectives: 8.07 us -> none  [local_step(): lax.all_gather(jnp.stack([local_max, local_sum, local_target]), 'tp')]
    reduce_sum x5 -> x0, other arithmetic: 6.96 us -> none  [the longest x3 3.64 us: rms_norm(): jnp.mean(vals_f32 * vals_f32, axis=-1, keepdims=True) + EPS]
    sub x1 -> x0, matrix products: 5.87 us -> none  [attention_block(): exp_scores = jnp.exp(scores - row_max)]
  transfers between devices with their start and end apart: 2 -> 0, of which waited for: 2 -> 0; matrix products, arithmetic and copies ran while one was open for 0% -> 0% of each run, Pallas kernels for 0% -> 0%
where the time goes in v1:
time: 103 us; the launch traced here: 102 us
  Pallas kernels  80.5 us (78%)
  local copies, waits for them, and re-layouts  20.3 us (20%)
    pallas_call x1, Pallas kernels, local_step(): pl.pallas_call(tail_kernel, out_shape=(jax.ShapeDtypeStruct((rows, width)...  71.2 us
    unnamed x21, local copies, waits for them, and re-layouts  15 us
    pallas_call x1, Pallas kernels, local_step(): pl.pallas_call(attention_kernel, out_shape=(jax.ShapeDtypeStruct((rows, w...  9.25 us

profile of v1, /device:TPU:0, one launch (start us, length us, event | category | flops | bytes accessed | tf_op | source)
XLA Modules:
  0.0 102.4 jit_solution(15610679405803672883)
XLA Ops:
  0.6 0.7 convert_element_type.3
  1.3 0.7 broadcast_in_dim.24.bq_ref
  2.0 0.7 broadcast_in_dim.23.g_ref
  2.7 1.3 %broadcast_in_dim.27.gm_ref = bf16[1,3072]{1,0:T(2,128)(2,1)} reshape(bf16[3072]{0:T(1024)(128)(2,1)} %param.32) | data formatting | bytes 12288 | tf_op jit(solution)/shard_map/broadcast_in_dim | solution.py:309
  4.0 1.3 %broadcast_in_dim.28.gf_ref = bf16[1,3072]{1,0:T(2,128)(2,1)} reshape(bf16[3072]{0:T(1024)(128)(2,1)} %param.36) | data formatting | bytes 12288 | tf_op jit(solution)/shard_map/broadcast_in_dim | solution.py:309
  5.3 1.4 %copy.24.tok_ref = s32[64,1]{1,0:T(8,128)} copy(s32[64,1]{0,1:T(1,128)} %bitcast.17) | data formatting | bytes 512 | tf_op jit(solution)/shard_map/broadcast_in_dim | solution.py:309
  6.6 0.2 fusion
  6.8 0.1 pad_maximum_fusion
  6.9 0.0 copy-start
  6.9 3.4 %copy-done = bf16[64,512,1,128]{3,1,2,0:T(8,128)(2,1)S(1)} copy-done((bf16[64,512,1,128]{3,1,2,0:T(8,128)(2,1)S(1)}, bf16[64,512,1,128]{3,1,2,0:T(8,128)(2,1)}, u32[]{:S(2)}) %copy-start) | copy-done | bytes 8388632
  10.3 1.7 %copy-done.1 = bf16[3072,384]{1,0:T(8,128)(2,1)S(1)} copy-done((bf16[3072,384]{1,0:T(8,128)(2,1)S(1)}, bf16[3072,384]{1,0:T(8,128)(2,1)}, u32[]{:S(2)}) %copy-start.1) | copy-done | bytes 2359320
  12.0 1.0 copy-done.2
  13.0 1.1 %copy-done.3 = bf16[3072,128]{1,0:T(8,128)(2,1)S(1)} copy-done((bf16[3072,128]{1,0:T(8,128)(2,1)S(1)}, bf16[3072,128]{1,0:T(8,128)(2,1)}, u32[]{:S(2)}) %copy-start.3) | copy-done | bytes 786456
  14.1 1.1 %copy-done.4 = bf16[3072,128]{1,0:T(8,128)(2,1)S(1)} copy-done((bf16[3072,128]{1,0:T(8,128)(2,1)S(1)}, bf16[3072,128]{1,0:T(8,128)(2,1)}, u32[]{:S(2)}) %copy-start.4) | copy-done | bytes 786456
  15.2 0.7 copy-done.6
  15.9 0.7 copy-done.7
  16.6 0.7 copy-done.8
  17.2 9.3 %attention.1 = (bf16[64,384]{1,0:T(8,128)(2,1)S(1)}, bf16[64,512,128]{2,1,0:T(8,128)(2,1)}, bf16[64,512,128]{2,1,0:T(8,128)(2,1)}) custom-call(s32[64]{0:T(128)S(1)} %copy-done.6, bf16[64,3072]{1,0:T(8,128)(2,1)S(1)} %copy-done.2, bf16[1,3072]{1,0:T(2,128)(2,1)S(1)} %broadcast_in_dim.23.g_ref, bf16[1,384]{1,0:T(2,128)(2,1)S(1)} %broadcast_in_dim.24.bq_ref, ...), custom_call_target="tpu_custom_call" | custom-call | tf_op jit(solution)/shard_map/attention/pallas_call | solution.py:274
  26.5 0.0 copy-start.5
  26.5 0.6 copy-done.5
  27.1 71.2 %tail.1 = (bf16[64,3072]{1,0:T(8,128)(2,1)}, f32[1,64]{1,0:T(1,128)}, f32[1,64]{1,0:T(1,128)}) custom-call(bf16[64,384]{1,0:T(8,128)(2,1)} %copy-done.5, bf16[64,3072]{1,0:T(8,128)(2,1)} %x_ref.3, bf16[1,3072]{1,0:T(2,128)(2,1)} %broadcast_in_dim.27.gm_ref, bf16[1,3072]{1,0:T(2,128)(2,1)} %broadcast_in_dim.28.gf_ref, s32[64,1]{1,0:T(8,128)} %copy.24.tok_ref, ...), custom_call_target="tpu_custom_call" | custom-call | tf_op jit(solution)/shard_map/tail/pallas_call | solution.py:292
  98.3 1.8 %copy.30 = bf16[64,3072]{1,0:T(8,128)(2,1)} copy(bf16[64,3072]{1,0:T(8,128)(2,1)} %get-tuple-element.32) | data formatting | bytes 786432
  100.1 1.2 %copy.31 = f32[64]{0:T(128)} copy(f32[64]{0:T(128)} %bitcast.21) | data formatting | bytes 512
  101.3 1.1 %copy.32 = f32[64]{0:T(128)} copy(f32[64]{0:T(128)} %bitcast.20) | data formatting | bytes 512
  (8 shorter events, 0.0 us)
Async XLA Ops:
  6.9 3.4 %copy-start = (bf16[64,512,1,128]{3,1,2,0:T(8,128)(2,1)S(1)}, bf16[64,512,1,128]{3,1,2,0:T(8,128)(2,1)}, u32[]{:S(2)}) copy-start(bf16[64,512,1,128]{3,1,2,0:T(8,128)(2,1)} %param.21) | copy-start | bytes 25165828
  10.3 1.7 %copy-start.1 = (bf16[3072,384]{1,0:T(8,128)(2,1)S(1)}, bf16[3072,384]{1,0:T(8,128)(2,1)}, u32[]{:S(2)}) copy-start(bf16[3072,384]{1,0:T(8,128)(2,1)} %wq_hbm.1) | copy-start | bytes 7077892
  12.0 1.0 copy-start.2
  13.0 1.1 %copy-start.3 = (bf16[3072,128]{1,0:T(8,128)(2,1)S(1)}, bf16[3072,128]{1,0:T(8,128)(2,1)}, u32[]{:S(2)}) copy-start(bf16[3072,128]{1,0:T(8,128)(2,1)} %wk_hbm.1) | copy-start | bytes 2359300
  14.1 1.1 %copy-start.4 = (bf16[3072,128]{1,0:T(8,128)(2,1)S(1)}, bf16[3072,128]{1,0:T(8,128)(2,1)}, u32[]{:S(2)}) copy-start(bf16[3072,128]{1,0:T(8,128)(2,1)} %wv_hbm.1) | copy-start | bytes 2359300
  15.2 0.7 copy-start.6
  15.9 0.7 copy-start.7
  16.6 0.7 copy-start.8
  26.5 0.6 copy-start.5

commit v2 on v0

v2 whole, which is shorter than its diff:
```python
import functools

import jax
import jax.numpy as jnp
import numpy as np
from jax import lax
from jax.experimental import pallas as pl
from jax.experimental.pallas import tpu as pltpu
from jax.sharding import PartitionSpec as P

THETA = 1000000.0
EPS = 1e-6
MESH = pl.DeviceIdType.MESH
GROUP_ROWS = 8
HEAD_ROWS = 512
HEAD_SLOTS = 9
DIAG, ACROSS_X, ACROSS_Y = (1, 1, 0), (0, 1, 0), (1, 0, 0)
SIBLING = (0, 0, 1)
CHIPS = (DIAG, ACROSS_X, ACROSS_Y)
FLIPS = ((1, 1, 0), (1, 1, 1), (0, 1, 0), (1, 0, 0), (0, 1, 1), (1, 0, 1), (0, 0, 1))
NT = (((1,), (1,)), ((), ()))
NN = (((1,), (0,)), ((), ()))
F32, BF16 = jnp.float32, jnp.bfloat16


def rms_scaled(out, first, vals_ref, gain_ref):
    vals = vals_ref[...].astype(F32)
    rows, width = vals.shape
    inv_rms = lax.rsqrt(jnp.mean(vals * vals, axis=-1, keepdims=True) + EPS)
    gain = gain_ref[...].astype(F32)
    for i in range(width // 128):
        cols = slice(i * 128, (i + 1) * 128)
        out[first:first + rows, cols] = (vals[:, cols] * inv_rms * gain[i:i + 1, :]).astype(BF16)


def dot(lhs, rhs, dims=NN):
    return lax.dot_general(lhs, rhs, dims, preferred_element_type=F32)


def attention_kernel(len_ref, freq_ref, g_ref, bq_ref, bk_ref, bv_ref, x_hbm, wq_hbm, wk_hbm, wv_hbm, kc_hbm, vc_hbm,
                     attn_ref, ko_hbm, vo_hbm,
                     x_ref, w_all, kbuf, vbuf, normed, q_scr, kn_scr, vn_scr, o_scr, len_col, w_sem, in_sem, out_sem):
    rows, cache_len, head_dim = kbuf.shape
    q_cols = wq_hbm.shape[1]
    heads = q_cols // head_dim
    groups = rows // GROUP_ROWS
    local = pltpu.make_async_copy
    x_copy = local(x_hbm, x_ref, w_sem.at[0])
    proj_copies = [
        local(wq_hbm, w_all.at[:, 0:q_cols], w_sem.at[1]),
        local(wk_hbm, w_all.at[:, q_cols:q_cols + head_dim], w_sem.at[2]),
        local(wv_hbm, w_all.at[:, q_cols + head_dim:q_cols + 2 * head_dim], w_sem.at[3]),
    ]
    x_copy.start()
    for copy in proj_copies:
        copy.start()

    def loads(g):
        rng = pl.ds(g * GROUP_ROWS, GROUP_ROWS)
        return local(kc_hbm.at[rng], kbuf.at[rng], in_sem.at[0, g]), local(vc_hbm.at[rng], vbuf.at[rng], in_sem.at[1, g])

    def stores(g):
        rng = pl.ds(g * GROUP_ROWS, GROUP_ROWS)
        return local(kbuf.at[rng], ko_hbm.at[rng], out_sem.at[0, g]), local(vbuf.at[rng], vo_hbm.at[rng], out_sem.at[1, g])

    for g in range(groups):
        for copy in loads(g):
            copy.start()

    for r in range(rows):
        len_col[r:r + 1, :] = jnp.full((1, head_dim), len_ref[r], jnp.int32).astype(F32)
    angles = len_col[...] * freq_ref[...]
    cos_part = jnp.cos(angles)
    lane = lax.broadcasted_iota(jnp.int32, (rows, head_dim), 1)
    sin_part = jnp.where(lane < head_dim // 2, -1.0, 1.0) * jnp.sin(angles)

    def rotate(vals):
        return vals * cos_part + pltpu.roll(vals, head_dim // 2, 1) * sin_part

    q_scr[...] = jnp.zeros_like(q_scr)
    x_copy.wait()
    rms_scaled(normed, 0, x_ref, g_ref)
    for copy in proj_copies:
        copy.wait()
    proj = dot(normed[...], w_all[...])
    for h in range(heads):
        q_scr[pl.ds(h, rows, stride=8), :] = rotate(proj[:, h * head_dim:(h + 1) * head_dim] + bq_ref[h:h + 1, :].astype(F32))
    kn_scr[...] = rotate(proj[:, q_cols:q_cols + head_dim] + bk_ref[...].astype(F32))
    vn_scr[...] = proj[:, q_cols + head_dim:q_cols + 2 * head_dim] + bv_ref[...].astype(F32)

    tile_ids = lax.broadcasted_iota(jnp.int32, (16, head_dim), 0)
    slot_ids = lax.broadcasted_iota(jnp.int32, (8, cache_len), 1)

    def patch(buf, new_ref, row, length):
        base = pl.multiple_of((length // 16) * 16, 16)
        tile = buf[row, pl.ds(base, 16), :].astype(F32)
        new = jnp.broadcast_to(new_ref[pl.ds(row, 1), :], tile.shape)
        buf[row, pl.ds(base, 16), :] = jnp.where(tile_ids == length - base, new, tile).astype(BF16)

    @pl.loop(0, groups)
    def group(g):
        for copy in loads(g):
            copy.wait()
        for j in range(GROUP_ROWS):
            row = g * GROUP_ROWS + j
            length = len_ref[row]
            patch(kbuf, kn_scr, row, length)
            patch(vbuf, vn_scr, row, length)
        for copy in stores(g):
            copy.start()
        probs = []
        for j in range(GROUP_ROWS):
            row = g * GROUP_ROWS + j
            q_row = q_scr[pl.ds(pl.multiple_of(row * 8, 8), 8), :].astype(BF16)
            scores = dot(q_row, kbuf[row], NT) * (head_dim ** -0.5)
            scores = jnp.where(slot_ids <= len_ref[row], scores, -jnp.inf)
            exp_scores = jnp.exp(scores - jnp.max(scores, axis=-1, keepdims=True))
            probs.append((exp_scores / jnp.sum(exp_scores, axis=-1, keepdims=True)).astype(BF16))
        for j in range(GROUP_ROWS):
            row = g * GROUP_ROWS + j
            o_scr[pl.ds(pl.multiple_of(row * 8, 8), 8), :] = dot(probs[j], vbuf[row])

    for h in range(heads):
        attn_ref[:, h * head_dim:(h + 1) * head_dim] = o_scr[pl.ds(h, rows, stride=8), :].astype(BF16)
    for g in range(groups):
        for copy in stores(g):
            copy.wait()


def tail_kernel(tok_ref, gm_ref, gf_ref, attn_ref, x_ref, wo_hbm, wg_hbm, wu_hbm, wd_hbm, wh_hbm,
                y_ref, stat_ref,
                wo, wg, wu, wd, ring, tok_col,
                send_buf, recv1, recv2, a_full, y_full, normed, gate_act, logits_a, logits_b, run_max, run_sum, run_tgt, stat_send, stat_recv,
                w_sem, ring_sem, send_sem, recv_sem):
    rows, width = x_ref.shape
    part = width // 8
    vocab = wh_hbm.shape[0]
    half_vocab = vocab // 2
    chunks = pl.cdiv(half_vocab, HEAD_ROWS)
    ff = wg.shape[1]
    me = lax.axis_index('tp')
    plane = lax.axis_index('dp')
    my_y, my_x, my_c = me // 4, (me // 2) % 2, me % 2

    def peer(flip):
        fy, fx, fc = flip
        pos_y = 1 - my_y if fy else my_y
        pos_x = 1 - my_x if fx else my_x
        pos_c = 1 - my_c if fc else my_c
        return pos_y * 4 + pos_x * 2 + pos_c

    def columns(who):
        return pl.ds(pl.multiple_of(who * part, 128), part)

    def local(src, dst, sem):
        return pltpu.make_async_copy(src, dst, sem)

    pending = []

    def remote(src, dst, stage, slot, device):
        return pltpu.make_async_remote_copy(
            src_ref=src, dst_ref=dst, send_sem=send_sem.at[stage, slot], recv_sem=recv_sem.at[stage, slot],
            device_id=device, device_id_type=MESH)

    def push(src, dst, stage, slot, device):
        copy = remote(src, dst, stage, slot, device)
        copy.start()
        pending.append(copy)
        return copy

    wo_copy = local(wo_hbm, wo, w_sem.at[0])
    wg_copy = local(wg_hbm, wg, w_sem.at[1])
    wu_copy = local(wu_hbm, wu, w_sem.at[2])
    wd_copy = local(wd_hbm, wd, w_sem.at[3])
    wo_copy.start()
    others = [{'tp': peer(flip)} for flip in FLIPS]
    others += [{'dp': 1 - plane, 'tp': peer(flip)} for flip in FLIPS + ((0, 0, 0),)]
    barrier = pltpu.get_barrier_semaphore()
    for device in others:
        pl.semaphore_signal(barrier, inc=1, device_id=device, device_id_type=MESH)

    for r in range(rows):
        tok_col[0, r:r + 1, :] = jnp.full((1, 128), tok_ref[r], jnp.int32)

    def head_copy(i):
        start = pl.multiple_of(plane * half_vocab + jnp.minimum(i * HEAD_ROWS, half_vocab - HEAD_ROWS), 16)
        slot = i % HEAD_SLOTS
        return local(wh_hbm.at[pl.ds(start, HEAD_ROWS)], ring.at[slot], ring_sem.at[slot])

    wo_copy.wait()
    wg_copy.start()
    wu_copy.start()
    wd_copy.start()
    for i in range(HEAD_SLOTS):
        head_copy(i).start()
    pl.semaphore_wait(barrier, len(others))
    push(tok_col.at[0], tok_col.at[1], 4, 15, {'dp': 1 - plane})

    def scatter_sum(stage, lhs, weight, recv, base):
        copies = []
        for k, flip in enumerate(FLIPS):
            who = peer(flip)
            send_buf[stage // 2, k] = dot(lhs, weight[:, columns(who)]).astype(BF16)
            copies.append(push(send_buf.at[stage // 2, k], recv.at[k], stage, k, {'tp': who}))
        total = dot(lhs, weight[:, columns(me)])
        for k in reversed(range(len(FLIPS))):
            copies[k].wait_recv()
            total = total + recv[k].astype(F32)
        return (base + total).astype(BF16)

    def gather(stage, full, planes):
        sibling = {'tp': peer(SIBLING)}

        def block(p, flip):
            return full.at[p, :, columns(peer(flip))]

        def move(p, flip, slot, device):
            push(block(p, flip), block(p, flip), stage, slot, device)

        def arrive(p, flip, slot):
            remote(block(p, flip), block(p, flip), stage, slot, sibling).wait_recv()

        own = (0, 0, 0)
        if planes == 2:
            push(block(0, own), block(1, own), stage, 14, {'dp': 1 - plane})
        for i, flip in enumerate(CHIPS):
            move(0, flip=own, slot=i, device={'tp': peer(flip)})
        move(0, own, 3, sibling)
        for p in range(planes):
            if p == 1:
                arrive(1, own, 14)
                for i, flip in enumerate(CHIPS):
                    move(1, own, 7 + i, {'tp': peer(flip)})
                move(1, own, 10, sibling)
        for p in range(planes):
            for i in (1, 2, 0):
                arrive(p, CHIPS[i], 7 * p + i)
                move(p, CHIPS[i], 7 * p + 4 + i, sibling)
        for p in range(planes):
            arrive(p, SIBLING, 7 * p + 3)
            for i in (1, 2, 0):
                fy, fx, _ = CHIPS[i]
                arrive(p, (fy, fx, 1), 7 * p + 4 + i)

    a_full[0, :, columns(me)] = scatter_sum(0, attn_ref[...], wo, recv1, x_ref[:, columns(me)].astype(F32))
    gather(1, a_full, 1)
    rms_scaled(normed, 0, a_full.at[0], gm_ref)
    wg_copy.wait()
    wu_copy.wait()

    @pl.loop(0, ff // 256)
    def mlp(i):
        cols = pl.ds(pl.multiple_of(i * 256, 256), 256)
        gate = dot(normed[0:rows], wg[:, cols])
        up = dot(normed[0:rows], wu[:, cols])
        gate_act[:, cols] = (jax.nn.silu(gate) * up).astype(BF16)

    wd_copy.wait()
    y_full[0, :, columns(me)] = scatter_sum(2, gate_act[...], wd, recv2, a_full[0, :, columns(me)].astype(F32))
    gather(3, y_full, 2)
    y_ref[...] = y_full[0]
    for p in range(2):
        rms_scaled(normed, p * rows, y_full.at[p], gf_ref)
    remote(tok_col.at[0], tok_col.at[1], 4, 15, {'dp': 1 - plane}).wait_recv()
    base = me * vocab + plane * half_vocab
    run_max[...] = jnp.full_like(run_max, -jnp.inf)
    run_sum[...] = jnp.zeros_like(run_sum)
    run_tgt[...] = jnp.zeros_like(run_tgt)
    lane_ids = lax.broadcasted_iota(jnp.int32, (16, 128), 1)

    def score(i, out):
        out[...] = dot(normed[...], ring[i % HEAD_SLOTS], NT)

    def absorb(i, logits):
        first = i * HEAD_ROWS
        start = jnp.minimum(first, half_vocab - HEAD_ROWS)
        for r in range(0, 2 * rows, 16):
            blk = slice(r, r + 16)
            local_tok = tok_col[r // rows, r % rows:r % rows + 16, :] - base
            old_max = run_max[blk]
            new_max = old_max
            tgt = run_tgt[blk]
            slabs = []
            for s in range(HEAD_ROWS // 128):
                ids = lane_ids + (start + s * 128)
                raw = logits[blk, s * 128:(s + 1) * 128]
                slab = jnp.where(ids >= first, raw, -jnp.inf)
                tgt = tgt + jnp.where(ids == jnp.where(local_tok >= first, local_tok, -1), raw, 0.0)
                new_max = jnp.maximum(new_max, slab)
                slabs.append(slab)
            total = run_sum[blk] * jnp.exp(old_max - new_max)
            for slab in slabs:
                total = total + jnp.exp(slab - new_max)
            run_max[blk] = new_max
            run_sum[blk] = total
            run_tgt[blk] = tgt

    def refill(i):
        @pl.when(i + HEAD_SLOTS < chunks)
        def _():
            head_copy(i + HEAD_SLOTS).start()

    head_copy(0).wait()
    score(0, logits_a)
    refill(0)

    @pl.loop(0, (chunks - 2) // 2)
    def head(pair):
        i = pair * 2 + 1
        head_copy(i).wait()
        head_copy(i + 1).wait()
        score(i, logits_b)
        absorb(i - 1, logits_a)
        score(i + 1, logits_a)
        absorb(i, logits_b)
        refill(i)
        refill(i + 1)

    head_copy(chunks - 1).wait()
    score(chunks - 1, logits_b)
    absorb(chunks - 2, logits_a)
    absorb(chunks - 1, logits_b)

    maxes = run_max[...]
    loc_max = jnp.max(maxes, axis=-1, keepdims=True)
    loc_sum = jnp.sum(run_sum[...] * jnp.exp(maxes - loc_max), axis=-1, keepdims=True)
    loc_tgt = jnp.sum(run_tgt[...], axis=-1, keepdims=True)
    lanes = lax.broadcasted_iota(jnp.int32, (2 * rows, 128), 1)
    own = jnp.transpose(jnp.where(lanes == 0, loc_max, jnp.where(lanes == 1, loc_sum, loc_tgt)))[0:8]
    stat_send[...] = own
    copies = [push(stat_send, stat_recv.at[k], 4, k, device) for k, device in enumerate(others)]
    stats = [own]
    for k, copy in enumerate(copies):
        copy.wait_recv()
        stats.append(stat_recv[k] if k < len(FLIPS) else pltpu.roll(stat_recv[k], rows, 1))
    glob_max = functools.reduce(jnp.maximum, [s[0:1] for s in stats])
    exp_total = functools.reduce(jnp.add, [s[1:2] * jnp.exp(s[0:1] - glob_max) for s in stats])
    stat_ref[0:1, :] = functools.reduce(jnp.add, [s[2:3] for s in stats])
    stat_ref[1:2, :] = glob_max + jnp.log(exp_total)
    for copy in pending:
        copy.wait_send()


def local_step(tok_hidden, seq_lens, k_cache, v_cache, next_tok, g_attn, w_q, b_q, w_k, b_k, w_v, b_v, w_o, g_mlp, w_gate, w_up, w_down, g_final, w_head):
    rows, width = tok_hidden.shape
    cache_shape = k_cache.shape
    cache_len, head_dim = cache_shape[1], cache_shape[3]
    flat = (rows, cache_len, head_dim)
    half_freq = np.power(np.float32(THETA), np.arange(head_dim // 2, dtype=np.float32) * np.float32(-2.0 / head_dim))
    freq = jnp.asarray(np.concatenate([half_freq, half_freq])[None].astype(np.float32))
    vmem = pl.BlockSpec(memory_space=pltpu.VMEM)
    smem = pl.BlockSpec(memory_space=pltpu.SMEM)
    hbm = pl.BlockSpec(memory_space=pltpu.HBM)
    groups = rows // GROUP_ROWS
    part = width // 8
    peers = len(FLIPS)
    attn_out, k_all, v_all = pl.pallas_call(
        attention_kernel,
        out_shape=(jax.ShapeDtypeStruct((rows, w_q.shape[1]), BF16), jax.ShapeDtypeStruct(flat, BF16), jax.ShapeDtypeStruct(flat, BF16)),
        in_specs=[smem] + [vmem] * 5 + [hbm] * 6,
        out_specs=(vmem, hbm, hbm),
        scratch_shapes=[
            pltpu.VMEM((rows, width), BF16), pltpu.VMEM((width, w_q.shape[1] + 2 * head_dim), BF16),
            pltpu.VMEM(flat, BF16), pltpu.VMEM(flat, BF16), pltpu.VMEM((rows, width), BF16),
            pltpu.VMEM((rows * 8, head_dim), F32), pltpu.VMEM((rows, head_dim), F32), pltpu.VMEM((rows, head_dim), F32),
            pltpu.VMEM((rows * 8, head_dim), F32), pltpu.VMEM((rows, head_dim), F32),
            pltpu.SemaphoreType.DMA((4,)), pltpu.SemaphoreType.DMA((2, groups)), pltpu.SemaphoreType.DMA((2, groups)),
        ],
        compiler_params=pltpu.CompilerParams(vmem_limit_bytes=67043328),
        name='attention',
    )(seq_lens, freq, g_attn.reshape(-1, 128), b_q.reshape(-1, 128), b_k.reshape(-1, 128), b_v.reshape(-1, 128),
      tok_hidden, w_q, w_k, w_v, k_cache.reshape(flat), v_cache.reshape(flat))
    y_out, stats = pl.pallas_call(
        tail_kernel,
        out_shape=(jax.ShapeDtypeStruct((rows, width), BF16), jax.ShapeDtypeStruct((8, 128), F32)),
        in_specs=[smem] + [vmem] * 4 + [hbm] * 5,
        out_specs=(vmem, vmem),
        scratch_shapes=[
            pltpu.VMEM(w_o.shape, BF16), pltpu.VMEM(w_gate.shape, BF16), pltpu.VMEM(w_up.shape, BF16), pltpu.VMEM(w_down.shape, BF16),
            pltpu.VMEM((HEAD_SLOTS, HEAD_ROWS, width), BF16), pltpu.VMEM((2, rows, 128), jnp.int32),
            pltpu.VMEM((2, peers, rows, part), BF16), pltpu.VMEM((peers, rows, part), BF16), pltpu.VMEM((peers, rows, part), BF16),
            pltpu.VMEM((1, rows, width), BF16), pltpu.VMEM((2, rows, width), BF16), pltpu.VMEM((2 * rows, width), BF16), pltpu.VMEM((rows, w_gate.shape[1]), BF16),
            pltpu.VMEM((2 * rows, HEAD_ROWS), F32), pltpu.VMEM((2 * rows, HEAD_ROWS), F32),
            pltpu.VMEM((2 * rows, 128), F32), pltpu.VMEM((2 * rows, 128), F32), pltpu.VMEM((2 * rows, 128), F32),
            pltpu.VMEM((8, 128), F32), pltpu.VMEM((2 * peers + 1, 8, 128), F32),
            pltpu.SemaphoreType.DMA((4,)), pltpu.SemaphoreType.DMA((HEAD_SLOTS,)),
            pltpu.SemaphoreType.DMA((5, 16)), pltpu.SemaphoreType.DMA((5, 16)),
        ],
        compiler_params=pltpu.CompilerParams(vmem_limit_bytes=60 * 1024 * 1024, collective_id=0, has_side_effects=True),
        name='tail',
    )(next_tok, g_mlp.reshape(-1, 128), g_final.reshape(-1, 128), attn_out, tok_hidden, w_o, w_gate, w_up, w_down, w_head)
    norm_lse = stats[1, :rows]
    return y_out, k_all.reshape(cache_shape), v_all.reshape(cache_shape), stats[0, :rows] - norm_lse, norm_lse


def solution(mesh):
    row_spec = P('dp', None)
    vec_spec = P('dp')
    cache_spec = P('dp', None, 'tp', None)
    col_spec = P(None, 'tp')
    part_spec = P('tp')
    whole_spec = P(None)
    in_specs = (row_spec, vec_spec, cache_spec, cache_spec, vec_spec, whole_spec, col_spec, part_spec, col_spec, part_spec, col_spec, part_spec, P('tp', None), whole_spec, col_spec, col_spec, P('tp', None), whole_spec, P('tp', None))
    out_specs = (row_spec, cache_spec, cache_spec, vec_spec, vec_spec)
    return jax.shard_map(local_step, mesh=mesh, in_specs=in_specs, out_specs=out_specs, check_vma=False)
```

time: 213 us -> 79.8 us (0.37)
  waiting for transfers between devices: 95.5 us -> 0 us
  Pallas kernels: 0 us -> 75.9 us
  matrix products: 70.4 us -> 0 us
  other arithmetic: 24.3 us -> 1.28 us
  between operations: 14.2 us -> 0.65 us
  blocking collectives: 8.07 us -> 0 us
    psum x2 -> x0, waiting for transfers between devices: 95.5 us -> none  [the longest x1 49.5 us: local_step(): attn_sum = lax.psum(attn_part, 'tp')]
    pallas_call x0 -> x2, Pallas kernels: none -> 75.9 us  [the longest x1 60 us: local_step(): pl.pallas_call(tail_kernel, out_shape=(jax.ShapeDtypeStruct((rows, width)...]
    dot_general x8 -> x0, matrix products: 64.5 us -> none  [the longest x1 41.3 us: local_step(): lax.dot_general(final_norm, w_head, (((1,), (1,)), ((), ())), preferred_e...]
    select_n x1 -> x0, other arithmetic: 11.9 us -> none  [attention_block(): k_all = jnp.where(write_mask, k_new[:, None], k_cache)]
    all_gather x1 -> x0, blocking collectives: 8.07 us -> none  [local_step(): lax.all_gather(jnp.stack([local_max, local_sum, local_target]), 'tp')]
    reduce_sum x5 -> x0, other arithmetic: 6.96 us -> none  [the longest x3 3.64 us: rms_norm(): jnp.mean(vals_f32 * vals_f32, axis=-1, keepdims=True) + EPS]
    sub x1 -> x0, matrix products: 5.87 us -> none  [attention_block(): exp_scores = jnp.exp(scores - row_max)]
    convert_element_type x7 -> x0, other arithmetic: 3.52 us -> none  [the longest x1 0.81 us: rotary(): angles = positions.astype(jnp.float32)[:, None] * inv_freq[None, :]]
  transfers between devices with their start and end apart: 2 -> 0, of which waited for: 2 -> 0; matrix products, arithmetic and copies ran while one was open for 0% -> 0% of each run, Pallas kernels for 0% -> 0%
where the time goes in v2:
time: 79.8 us; the launch traced here: 79.6 us
  Pallas kernels  75.9 us (95%)
  local copies, waits for them, and re-layouts  1.77 us (2%)
  other arithmetic  1.28 us (2%)
    pallas_call x1, Pallas kernels, local_step(): pl.pallas_call(tail_kernel, out_shape=(jax.ShapeDtypeStruct((rows, width)...  60 us
    pallas_call x1, Pallas kernels, local_step(): pl.pallas_call(attention_kernel, out_shape=(jax.ShapeDtypeStruct((rows, w...  15.9 us
    unnamed x1, local copies, waits for them, and re-layouts  1.77 us

profile of v2, /device:TPU:0, one launch (start us, length us, event | category | flops | bytes accessed | tf_op | source)
XLA Modules:
  0.0 79.6 jit_solution(8307254901290799858)
XLA Ops:
  0.6 15.9 %attention.1 = (bf16[64,384]{1,0:T(8,128)(2,1)}, bf16[64,512,128]{2,1,0:T(8,128)(2,1)}, bf16[64,512,128]{2,1,0:T(8,128)(2,1)}) custom-call(s32[64]{0:T(128)} %len_ref.1, f32[1,128]{1,0:T(1,128)} %constant.2.clone.freq_ref, bf16[24,128]{1,0:T(8,128)(2,1)} %bitcast.21, bf16[3,128]{1,0:T(4,128)(2,1)} %bitcast.24, bf16[1,128]{1,0:T(2,128)(2,1)} %bitcast.25, ...), custom_call_target="tpu_custom_call" | custom-call | tf_op jit(solution)/shard_map/attention/pallas_call | solution.py:357
  16.5 60.0 %tail.1 = (bf16[64,3072]{1,0:T(8,128)(2,1)}, f32[8,128]{1,0:T(8,128)}) custom-call(s32[64]{0:T(128)} %tok_ref.1, bf16[24,128]{1,0:T(8,128)(2,1)} %bitcast.22, bf16[24,128]{1,0:T(8,128)(2,1)} %bitcast.23, bf16[64,384]{1,0:T(8,128)(2,1)} %get-tuple-element.10.attn_ref, bf16[64,3072]{1,0:T(8,128)(2,1)} %x_ref.1, bf16[384,3072]{1,0:T(8,128)(2,1)} %wo_hbm.1, ...), custom_call_target="tpu_custom_call" | custom-call | tf_op jit(solution)/shard_map/tail/pallas_call | solution.py:373
  76.5 1.3 %bitcast_subtract_fusion = (f32[64]{0:T(128)}, f32[64]{0:T(128)}) fusion(f32[8,128]{1,0:T(8,128)} %get-tuple-element.14), kind=kLoop, calls=%fused_computation | loop fusion | flops 64 | bytes 1024 | tf_op jit(solution)/shard_map/sub | solution.py:393
  77.8 1.8 %copy.28 = bf16[64,3072]{1,0:T(8,128)(2,1)} copy(bf16[64,3072]{1,0:T(8,128)(2,1)} %get-tuple-element.27) | data formatting | bytes 786432

commit v3 on v2

--- a/solution.py
+++ b/solution.py
@@ -14,9 +14,11 @@
 GROUP_ROWS = 8
 HEAD_ROWS = 512
 HEAD_SLOTS = 9
+EARLY_GROUPS = 2
 DIAG, ACROSS_X, ACROSS_Y = (1, 1, 0), (0, 1, 0), (1, 0, 0)
 SIBLING = (0, 0, 1)
 CHIPS = (DIAG, ACROSS_X, ACROSS_Y)
+OWN = (0, 0, 0)
 FLIPS = ((1, 1, 0), (1, 1, 1), (0, 1, 0), (1, 0, 0), (0, 1, 1), (1, 0, 1), (0, 0, 1))
 NT = (((1,), (1,)), ((), ()))
 NN = (((1,), (0,)), ((), ()))
@@ -37,22 +39,25 @@
     return lax.dot_general(lhs, rhs, dims, preferred_element_type=F32)
 
 
-def attention_kernel(len_ref, freq_ref, g_ref, bq_ref, bk_ref, bv_ref, x_hbm, wq_hbm, wk_hbm, wv_hbm, kc_hbm, vc_hbm,
-                     attn_ref, ko_hbm, vo_hbm,
-                     x_ref, w_all, kbuf, vbuf, normed, q_scr, kn_scr, vn_scr, o_scr, len_col, w_sem, in_sem, out_sem):
+def attention_kernel(len_hbm, freq_hbm, g_hbm, bq_hbm, bk_hbm, bv_hbm, x_hbm, wq_hbm, wk_hbm, wv_hbm, kc_hbm, vc_hbm, wo_hbm,
+                     part_hbm, ko_hbm, vo_hbm,
+                     len_ref, freq_ref, g_ref, bq_ref, bk_ref, bv_ref, x_ref, w_all, wo, kbuf, vbuf, normed, q_scr, kn_scr, vn_scr, o_scr, len_col, part_scr,
+                     w_sem, in_sem, out_sem):
     rows, cache_len, head_dim = kbuf.shape
     q_cols = wq_hbm.shape[1]
     heads = q_cols // head_dim
     groups = rows // GROUP_ROWS
     local = pltpu.make_async_copy
-    x_copy = local(x_hbm, x_ref, w_sem.at[0])
+    small = [local(src, dst, w_sem.at[i]) for i, (src, dst) in enumerate((
+        (x_hbm, x_ref), (len_hbm, len_ref), (freq_hbm, freq_ref), (g_hbm, g_ref), (bq_hbm, bq_ref), (bk_hbm, bk_ref), (bv_hbm, bv_ref)))]
     proj_copies = [
-        local(wq_hbm, w_all.at[:, 0:q_cols], w_sem.at[1]),
-        local(wk_hbm, w_all.at[:, q_cols:q_cols + head_dim], w_sem.at[2]),
-        local(wv_hbm, w_all.at[:, q_cols + head_dim:q_cols + 2 * head_dim], w_sem.at[3]),
+        local(wq_hbm, w_all.at[:, 0:q_cols], w_sem.at[7]),
+        local(wk_hbm, w_all.at[:, q_cols:q_cols + head_dim], w_sem.at[8]),
+        local(wv_hbm, w_all.at[:, q_cols + head_dim:q_cols + 2 * head_dim], w_sem.at[9]),
     ]
-    x_copy.start()
-    for copy in proj_copies:
+    wo_copy = local(wo_hbm, wo, w_sem.at[10])
+    part_copy = local(part_scr, part_hbm, w_sem.at[11])
+    for copy in small + proj_copies:
         copy.start()
 
     def loads(g):
@@ -63,10 +68,11 @@
         rng = pl.ds(g * GROUP_ROWS, GROUP_ROWS)
         return local(kbuf.at[rng], ko_hbm.at[rng], out_sem.at[0, g]), local(vbuf.at[rng], vo_hbm.at[rng], out_sem.at[1, g])
 
-    for g in range(groups):
+    for g in range(EARLY_GROUPS):
         for copy in loads(g):
             copy.start()
-
+    for copy in small:
+        copy.wait()
     for r in range(rows):
         len_col[r:r + 1, :] = jnp.full((1, head_dim), len_ref[r], jnp.int32).astype(F32)
     angles = len_col[...] * freq_ref[...]
@@ -78,10 +84,13 @@
         return vals * cos_part + pltpu.roll(vals, head_dim // 2, 1) * sin_part
 
     q_scr[...] = jnp.zeros_like(q_scr)
-    x_copy.wait()
     rms_scaled(normed, 0, x_ref, g_ref)
     for copy in proj_copies:
         copy.wait()
+    for g in range(EARLY_GROUPS, groups):
+        for copy in loads(g):
+            copy.start()
+    wo_copy.start()
     proj = dot(normed[...], w_all[...])
     for h in range(heads):
         q_scr[pl.ds(h, rows, stride=8), :] = rotate(proj[:, h * head_dim:(h + 1) * head_dim] + bq_ref[h:h + 1, :].astype(F32))
@@ -120,24 +129,30 @@
             row = g * GROUP_ROWS + j
             o_scr[pl.ds(pl.multiple_of(row * 8, 8), 8), :] = dot(probs[j], vbuf[row])
 
-    for h in range(heads):
-        attn_ref[:, h * head_dim:(h + 1) * head_dim] = o_scr[pl.ds(h, rows, stride=8), :].astype(BF16)
+    attn = jnp.concatenate([o_scr[pl.ds(h, rows, stride=8), :].astype(BF16) for h in range(heads)], axis=1)
+    wo_copy.wait()
+    part = part_scr.shape[2]
+    for d in range(part_scr.shape[0]):
+        part_scr[d] = dot(attn, wo[:, d * part:(d + 1) * part]).astype(BF16)
+    part_copy.start()
     for g in range(groups):
         for copy in stores(g):
             copy.wait()
-
-
-def tail_kernel(tok_ref, gm_ref, gf_ref, attn_ref, x_ref, wo_hbm, wg_hbm, wu_hbm, wd_hbm, wh_hbm,
+    part_copy.wait()
+
+
+def tail_kernel(tok_hbm, gm_hbm, gf_hbm, part_hbm, x_hbm, wg_hbm, wu_hbm, wd_hbm, wh_hbm,
                 y_ref, stat_ref,
-                wo, wg, wu, wd, ring, tok_col,
-                send_buf, recv1, recv2, a_full, y_full, normed, gate_act, logits_a, logits_b, run_max, run_sum, run_tgt, stat_send, stat_recv,
+                tok_ref, gm_ref, gf_ref, part_ref, x_ref, wg, wu, ring, tok_col,
+                down_ref, half_recv, chip_send, chip_recv, a_full, y_full, normed, gate_act, logits_a, logits_b, run_max, run_sum, run_tgt, stat_send, stat_recv,
                 w_sem, ring_sem, send_sem, recv_sem):
-    rows, width = x_ref.shape
-    part = width // 8
+    rows, part = x_ref.shape
+    width = part * 8
     vocab = wh_hbm.shape[0]
     half_vocab = vocab // 2
     chunks = pl.cdiv(half_vocab, HEAD_ROWS)
     ff = wg.shape[1]
+    spare = HEAD_SLOTS - ff // HEAD_ROWS
     me = lax.axis_index('tp')
     plane = lax.axis_index('dp')
     my_y, my_x, my_c = me // 4, (me // 2) % 2, me % 2
@@ -168,49 +183,55 @@
         pending.append(copy)
         return copy
 
-    wo_copy = local(wo_hbm, wo, w_sem.at[0])
-    wg_copy = local(wg_hbm, wg, w_sem.at[1])
-    wu_copy = local(wu_hbm, wu, w_sem.at[2])
-    wd_copy = local(wd_hbm, wd, w_sem.at[3])
-    wo_copy.start()
+    small = [local(src, dst, w_sem.at[i]) for i, (src, dst) in enumerate((
+        (part_hbm, part_ref), (x_hbm.at[:, columns(me)], x_ref), (tok_hbm, tok_ref), (gm_hbm, gm_ref), (gf_hbm, gf_ref)))]
+    wg_copy = local(wg_hbm, wg, w_sem.at[5])
+    wu_copy = local(wu_hbm, wu, w_sem.at[6])
+    wd_copies = [local(wd_hbm.at[pl.ds(i * HEAD_ROWS, HEAD_ROWS)], ring.at[spare + i], ring_sem.at[spare + i]) for i in range(ff // HEAD_ROWS)]
+    for copy in small:
+        copy.start()
+    wg_copy.start()
+    wu_copy.start()
     others = [{'tp': peer(flip)} for flip in FLIPS]
     others += [{'dp': 1 - plane, 'tp': peer(flip)} for flip in FLIPS + ((0, 0, 0),)]
     barrier = pltpu.get_barrier_semaphore()
     for device in others:
         pl.semaphore_signal(barrier, inc=1, device_id=device, device_id_type=MESH)
 
-    for r in range(rows):
-        tok_col[0, r:r + 1, :] = jnp.full((1, 128), tok_ref[r], jnp.int32)
-
     def head_copy(i):
         start = pl.multiple_of(plane * half_vocab + jnp.minimum(i * HEAD_ROWS, half_vocab - HEAD_ROWS), 16)
         slot = i % HEAD_SLOTS
         return local(wh_hbm.at[pl.ds(start, HEAD_ROWS)], ring.at[slot], ring_sem.at[slot])
 
-    wo_copy.wait()
-    wg_copy.start()
-    wu_copy.start()
-    wd_copy.start()
-    for i in range(HEAD_SLOTS):
-        head_copy(i).start()
+    for copy in small:
+        copy.wait()
+    for r in range(rows):
+        tok_col[0, r:r + 1, :] = jnp.full((1, 128), tok_ref[r], jnp.int32)
     pl.semaphore_wait(barrier, len(others))
     push(tok_col.at[0], tok_col.at[1], 4, 15, {'dp': 1 - plane})
 
-    def scatter_sum(stage, lhs, weight, recv, base):
+    sibling = {'tp': peer(SIBLING)}
+
+    def scatter_sum(stage, source, base):
+        halves = []
+        for i, (fy, fx, _) in enumerate(CHIPS + (OWN,)):
+            source(peer((fy, fx, 1)), i, True)
+            src = part_ref.at[peer((fy, fx, 1))] if stage == 0 else down_ref.at[i]
+            halves.append(push(src, half_recv.at[stage // 2, i], stage, i, sibling))
+        mine = [source(peer(flip), i, False) for i, flip in enumerate(CHIPS + (OWN,))]
         copies = []
-        for k, flip in enumerate(FLIPS):
-            who = peer(flip)
-            send_buf[stage // 2, k] = dot(lhs, weight[:, columns(who)]).astype(BF16)
-            copies.append(push(send_buf.at[stage // 2, k], recv.at[k], stage, k, {'tp': who}))
-        total = dot(lhs, weight[:, columns(me)])
-        for k in reversed(range(len(FLIPS))):
-            copies[k].wait_recv()
-            total = total + recv[k].astype(F32)
+        for i, flip in enumerate(CHIPS):
+            halves[i].wait_recv()
+            chip_send[stage // 2, i] = (mine[i] + half_recv[stage // 2, i].astype(F32)).astype(BF16)
+            copies.append(push(chip_send.at[stage // 2, i], chip_recv.at[stage // 2, i], stage, 4 + i, {'tp': peer(flip)}))
+        halves[3].wait_recv()
+        total = mine[3] + half_recv[stage // 2, 3].astype(F32)
+        for i in (1, 2, 0):
+            copies[i].wait_recv()
+            total = total + chip_recv[stage // 2, i].astype(F32)
         return (base + total).astype(BF16)
 
     def gather(stage, full, planes):
-        sibling = {'tp': peer(SIBLING)}
-
         def block(p, flip):
             return full.at[p, :, columns(peer(flip))]
 
@@ -220,7 +241,7 @@
         def arrive(p, flip, slot):
             remote(block(p, flip), block(p, flip), stage, slot, sibling).wait_recv()
 
-        own = (0, 0, 0)
+        own = OWN
         if planes == 2:
             push(block(0, own), block(1, own), stage, 14, {'dp': 1 - plane})
         for i, flip in enumerate(CHIPS):
@@ -242,8 +263,15 @@
                 fy, fx, _ = CHIPS[i]
                 arrive(p, (fy, fx, 1), 7 * p + 4 + i)
 
-    a_full[0, :, columns(me)] = scatter_sum(0, attn_ref[...], wo, recv1, x_ref[:, columns(me)].astype(F32))
+    def attn_source(who, i, send):
+        return None if send else part_ref[who].astype(F32)
+
+    a_full[0, :, columns(me)] = scatter_sum(0, attn_source, x_ref[...].astype(F32))
+    for copy in wd_copies:
+        copy.start()
     gather(1, a_full, 1)
+    for i in range(3):
+        head_copy(i).start()
     rms_scaled(normed, 0, a_full.at[0], gm_ref)
     wg_copy.wait()
     wu_copy.wait()
@@ -255,8 +283,23 @@
         up = dot(normed[0:rows], wu[:, cols])
         gate_act[:, cols] = (jax.nn.silu(gate) * up).astype(BF16)
 
-    wd_copy.wait()
-    y_full[0, :, columns(me)] = scatter_sum(2, gate_act[...], wd, recv2, a_full[0, :, columns(me)].astype(F32))
+    for i in range(3, spare):
+        head_copy(i).start()
+    for copy in wd_copies:
+        copy.wait()
+
+    def down_source(who, i, send):
+        out = None
+        for j in range(ff // HEAD_ROWS):
+            term = dot(gate_act[:, j * HEAD_ROWS:(j + 1) * HEAD_ROWS], ring[spare + j, :, columns(who)])
+            out = term if out is None else out + term
+        if send:
+            down_ref[i] = out.astype(BF16)
+        return out
+
+    y_full[0, :, columns(me)] = scatter_sum(2, down_source, a_full[0, :, columns(me)].astype(F32))
+    for i in range(spare, HEAD_SLOTS):
+        head_copy(i).start()
     gather(3, y_full, 2)
     y_ref[...] = y_full[0]
     for p in range(2):
@@ -349,46 +392,48 @@
     half_freq = np.power(np.float32(THETA), np.arange(head_dim // 2, dtype=np.float32) * np.float32(-2.0 / head_dim))
     freq = jnp.asarray(np.concatenate([half_freq, half_freq])[None].astype(np.float32))
     vmem = pl.BlockSpec(memory_space=pltpu.VMEM)
-    smem = pl.BlockSpec(memory_space=pltpu.SMEM)
     hbm = pl.BlockSpec(memory_space=pltpu.HBM)
     groups = rows // GROUP_ROWS
     part = width // 8
     peers = len(FLIPS)
-    attn_out, k_all, v_all = pl.pallas_call(
+    attn_part, k_all, v_all = pl.pallas_call(
         attention_kernel,
-        out_shape=(jax.ShapeDtypeStruct((rows, w_q.shape[1]), BF16), jax.ShapeDtypeStruct(flat, BF16), jax.ShapeDtypeStruct(flat, BF16)),
-        in_specs=[smem] + [vmem] * 5 + [hbm] * 6,
-        out_specs=(vmem, hbm, hbm),
+        out_shape=(jax.ShapeDtypeStruct((8, rows, part), BF16), jax.ShapeDtypeStruct(flat, BF16), jax.ShapeDtypeStruct(flat, BF16)),
+        in_specs=[hbm] * 13,
+        out_specs=(hbm, hbm, hbm),
         scratch_shapes=[
-            pltpu.VMEM((rows, width), BF16), pltpu.VMEM((width, w_q.shape[1] + 2 * head_dim), BF16),
+            pltpu.SMEM((rows,), jnp.int32), pltpu.VMEM((1, head_dim), F32), pltpu.VMEM((width // 128, 128), BF16),
+            pltpu.VMEM((w_q.shape[1] // 128, 128), BF16), pltpu.VMEM((1, 128), BF16), pltpu.VMEM((1, 128), BF16),
+            pltpu.VMEM((rows, width), BF16), pltpu.VMEM((width, w_q.shape[1] + 2 * head_dim), BF16), pltpu.VMEM(w_o.shape, BF16),
             pltpu.VMEM(flat, BF16), pltpu.VMEM(flat, BF16), pltpu.VMEM((rows, width), BF16),
             pltpu.VMEM((rows * 8, head_dim), F32), pltpu.VMEM((rows, head_dim), F32), pltpu.VMEM((rows, head_dim), F32),
-            pltpu.VMEM((rows * 8, head_dim), F32), pltpu.VMEM((rows, head_dim), F32),
-            pltpu.SemaphoreType.DMA((4,)), pltpu.SemaphoreType.DMA((2, groups)), pltpu.SemaphoreType.DMA((2, groups)),
+            pltpu.VMEM((rows * 8, head_dim), F32), pltpu.VMEM((rows, head_dim), F32), pltpu.VMEM((8, rows, part), BF16),
+            pltpu.SemaphoreType.DMA((12,)), pltpu.SemaphoreType.DMA((2, groups)), pltpu.SemaphoreType.DMA((2, groups)),
         ],
         compiler_params=pltpu.CompilerParams(vmem_limit_bytes=67043328),
         name='attention',
     )(seq_lens, freq, g_attn.reshape(-1, 128), b_q.reshape(-1, 128), b_k.reshape(-1, 128), b_v.reshape(-1, 128),
-      tok_hidden, w_q, w_k, w_v, k_cache.reshape(flat), v_cache.reshape(flat))
+      tok_hidden, w_q, w_k, w_v, k_cache.reshape(flat), v_cache.reshape(flat), w_o)
     y_out, stats = pl.pallas_call(
         tail_kernel,
         out_shape=(jax.ShapeDtypeStruct((rows, width), BF16), jax.ShapeDtypeStruct((8, 128), F32)),
-        in_specs=[smem] + [vmem] * 4 + [hbm] * 5,
+        in_specs=[hbm] * 9,
         out_specs=(vmem, vmem),
         scratch_shapes=[
-            pltpu.VMEM(w_o.shape, BF16), pltpu.VMEM(w_gate.shape, BF16), pltpu.VMEM(w_up.shape, BF16), pltpu.VMEM(w_down.shape, BF16),
+            pltpu.SMEM((rows,), jnp.int32), pltpu.VMEM((width // 128, 128), BF16), pltpu.VMEM((width // 128, 128), BF16),
+            pltpu.VMEM((8, rows, part), BF16), pltpu.VMEM((rows, part), BF16), pltpu.VMEM(w_gate.shape, BF16), pltpu.VMEM(w_up.shape, BF16),
             pltpu.VMEM((HEAD_SLOTS, HEAD_ROWS, width), BF16), pltpu.VMEM((2, rows, 128), jnp.int32),
-            pltpu.VMEM((2, peers, rows, part), BF16), pltpu.VMEM((peers, rows, part), BF16), pltpu.VMEM((peers, rows, part), BF16),
+            pltpu.VMEM((4, rows, part), BF16), pltpu.VMEM((2, 4, rows, part), BF16), pltpu.VMEM((2, 3, rows, part), BF16), pltpu.VMEM((2, 3, rows, part), BF16),
             pltpu.VMEM((1, rows, width), BF16), pltpu.VMEM((2, rows, width), BF16), pltpu.VMEM((2 * rows, width), BF16), pltpu.VMEM((rows, w_gate.shape[1]), BF16),
             pltpu.VMEM((2 * rows, HEAD_ROWS), F32), pltpu.VMEM((2 * rows, HEAD_ROWS), F32),
             pltpu.VMEM((2 * rows, 128), F32), pltpu.VMEM((2 * rows, 128), F32), pltpu.VMEM((2 * rows, 128), F32),
             pltpu.VMEM((8, 128), F32), pltpu.VMEM((2 * peers + 1, 8, 128), F32),
-            pltpu.SemaphoreType.DMA((4,)), pltpu.SemaphoreType.DMA((HEAD_SLOTS,)),
+            pltpu.SemaphoreType.DMA((7,)), pltpu.SemaphoreType.DMA((HEAD_SLOTS,)),
             pltpu.SemaphoreType.DMA((5, 16)), pltpu.SemaphoreType.DMA((5, 16)),
         ],
-        compiler_params=pltpu.CompilerParams(vmem_limit_bytes=60 * 1024 * 1024, collective_id=0, has_side_effects=True),
+        compiler_params=pltpu.CompilerParams(vmem_limit_bytes=57 * 1024 * 1024, collective_id=0, has_side_effects=True),
         name='tail',
-    )(next_tok, g_mlp.reshape(-1, 128), g_final.reshape(-1, 128), attn_out, tok_hidden, w_o, w_gate, w_up, w_down, w_head)
+    )(next_tok, g_mlp.reshape(-1, 128), g_final.reshape(-1, 128), attn_part, tok_hidden, w_gate, w_up, w_down, w_head)
     norm_lse = stats[1, :rows]
     return y_out, k_all.reshape(cache_shape), v_all.reshape(cache_shape), stats[0, :rows] - norm_lse, norm_lse
 

time: 79.8 us -> 77.8 us (0.975)
  Pallas kernels: 75.9 us -> 73.9 us
    pallas_call x1, Pallas kernels: 60 us -> 57.2 us  [local_step(): pl.pallas_call(tail_kernel, out_shape=(jax.ShapeDtypeStruct((rows, width)...]
    pallas_call x1, Pallas kernels: 15.9 us -> 16.8 us  [local_step(): pl.pallas_call(attention_kernel, out_shape=(jax.ShapeDtypeStruct((8, rows...]
where the time goes in v3:
time: 77.8 us; the launch traced here: 77.6 us
  Pallas kernels  73.9 us (95%)
  local copies, waits for them, and re-layouts  1.77 us (2%)
  other arithmetic  1.28 us (2%)
    pallas_call x1, Pallas kernels, local_step(): pl.pallas_call(tail_kernel, out_shape=(jax.ShapeDtypeStruct((rows, width)...  57.2 us
    pallas_call x1, Pallas kernels, local_step(): pl.pallas_call(attention_kernel, out_shape=(jax.ShapeDtypeStruct((8, rows...  16.8 us
    unnamed x1, local copies, waits for them, and re-layouts  1.77 us

profile of v3, /device:TPU:0, one launch (start us, length us, event | category | flops | bytes accessed | tf_op | source)
XLA Modules:
  0.0 77.6 jit_solution(9865333522573493427)
XLA Ops:
  0.6 16.8 %attention.1 = (bf16[8,64,384]{2,1,0:T(8,128)(2,1)}, bf16[64,512,128]{2,1,0:T(8,128)(2,1)}, bf16[64,512,128]{2,1,0:T(8,128)(2,1)}) custom-call(s32[64]{0:T(128)} %len_hbm.1, f32[1,128]{1,0:T(1,128)} %constant.2.clone.freq_hbm, bf16[24,128]{1,0:T(8,128)(2,1)} %bitcast.21, bf16[3,128]{1,0:T(4,128)(2,1)} %bitcast.24, bf16[1,128]{1,0:T(2,128)(2,1)} %bitcast.25, ...), custom_call_target="tpu_custom_call" | custom-call | tf_op jit(solution)/shard_map/attention/pallas_call | solution.py:399
  17.4 57.2 %tail.1 = (bf16[64,3072]{1,0:T(8,128)(2,1)}, f32[8,128]{1,0:T(8,128)}) custom-call(s32[64]{0:T(128)} %tok_hbm.1, bf16[24,128]{1,0:T(8,128)(2,1)} %bitcast.22, bf16[24,128]{1,0:T(8,128)(2,1)} %bitcast.23, bf16[8,64,384]{2,1,0:T(8,128)(2,1)} %get-tuple-element.10.part_hbm, bf16[64,3072]{1,0:T(8,128)(2,1)} %x_hbm.3, bf16[3072,1024]{1,0:T(8,128)(2,1)} %wg_hbm.1, ...), custom_call_target="tpu_custom_call" | custom-call | tf_op jit(solution)/shard_map/tail/pallas_call | solution.py:417
  74.6 1.3 %bitcast_subtract_fusion = (f32[64]{0:T(128)}, f32[64]{0:T(128)}) fusion(f32[8,128]{1,0:T(8,128)} %get-tuple-element.14), kind=kLoop, calls=%fused_computation | loop fusion | flops 64 | bytes 1024 | tf_op jit(solution)/shard_map/sub | solution.py:438
  75.8 1.8 %copy.28 = bf16[64,3072]{1,0:T(8,128)(2,1)} copy(bf16[64,3072]{1,0:T(8,128)(2,1)} %get-tuple-element.27) | data formatting | bytes 786432

commit v4 on v3

--- a/solution.py
+++ b/solution.py
@@ -14,7 +14,6 @@
 GROUP_ROWS = 8
 HEAD_ROWS = 512
 HEAD_SLOTS = 9
-EARLY_GROUPS = 2
 DIAG, ACROSS_X, ACROSS_Y = (1, 1, 0), (0, 1, 0), (1, 0, 0)
 SIBLING = (0, 0, 1)
 CHIPS = (DIAG, ACROSS_X, ACROSS_Y)
@@ -25,23 +24,24 @@
 F32, BF16 = jnp.float32, jnp.bfloat16
 
 
-def rms_scaled(out, first, vals_ref, gain_ref):
-    vals = vals_ref[...].astype(F32)
-    rows, width = vals.shape
-    inv_rms = lax.rsqrt(jnp.mean(vals * vals, axis=-1, keepdims=True) + EPS)
+def rms_scaled(out, first, blocks, gain_ref):
+    vals = [block.astype(F32) for block in blocks]
+    rows, part = vals[0].shape
+    squares = functools.reduce(jnp.add, [v * v for v in vals])
+    inv_rms = lax.rsqrt(jnp.sum(squares, axis=-1, keepdims=True) / (part * len(vals)) + EPS)
     gain = gain_ref[...].astype(F32)
-    for i in range(width // 128):
-        cols = slice(i * 128, (i + 1) * 128)
-        out[first:first + rows, cols] = (vals[:, cols] * inv_rms * gain[i:i + 1, :]).astype(BF16)
+    for i in range(part * len(vals) // 128):
+        block, lane = divmod(i * 128, part)
+        out[first:first + rows, i * 128:(i + 1) * 128] = (vals[block][:, lane:lane + 128] * inv_rms * gain[i:i + 1, :]).astype(BF16)
 
 
 def dot(lhs, rhs, dims=NN):
     return lax.dot_general(lhs, rhs, dims, preferred_element_type=F32)
 
 
-def attention_kernel(len_hbm, freq_hbm, g_hbm, bq_hbm, bk_hbm, bv_hbm, x_hbm, wq_hbm, wk_hbm, wv_hbm, kc_hbm, vc_hbm, wo_hbm,
+def attention_kernel(len_hbm, tok_hbm, freq_hbm, g_hbm, gm_hbm, gf_hbm, bq_hbm, bk_hbm, bv_hbm, x_hbm, wq_hbm, wk_hbm, wv_hbm, kc_hbm, vc_hbm, wo_hbm,
                      part_hbm, ko_hbm, vo_hbm,
-                     len_ref, freq_ref, g_ref, bq_ref, bk_ref, bv_ref, x_ref, w_all, wo, kbuf, vbuf, normed, q_scr, kn_scr, vn_scr, o_scr, len_col, part_scr,
+                     len_ref, tok_ref, freq_ref, g_ref, bq_ref, bk_ref, bv_ref, x_ref, wq, wk, wv, wo, kbuf, vbuf, normed, q_scr, kn_scr, vn_scr, o_scr, len_col, part_scr,
                      w_sem, in_sem, out_sem):
     rows, cache_len, head_dim = kbuf.shape
     q_cols = wq_hbm.shape[1]
@@ -49,14 +49,16 @@
     groups = rows // GROUP_ROWS
     local = pltpu.make_async_copy
     small = [local(src, dst, w_sem.at[i]) for i, (src, dst) in enumerate((
-        (x_hbm, x_ref), (len_hbm, len_ref), (freq_hbm, freq_ref), (g_hbm, g_ref), (bq_hbm, bq_ref), (bk_hbm, bk_ref), (bv_hbm, bv_ref)))]
+        (x_hbm, x_ref), (len_hbm, len_ref), (freq_hbm, freq_ref), (g_hbm, g_ref), (bq_hbm, bq_ref), (bk_hbm, bk_ref), (bv_hbm, bv_ref), (tok_hbm, tok_ref)))]
     proj_copies = [
-        local(wq_hbm, w_all.at[:, 0:q_cols], w_sem.at[7]),
-        local(wk_hbm, w_all.at[:, q_cols:q_cols + head_dim], w_sem.at[8]),
-        local(wv_hbm, w_all.at[:, q_cols + head_dim:q_cols + 2 * head_dim], w_sem.at[9]),
+        local(wq_hbm, wq, w_sem.at[8]),
+        local(wk_hbm, wk, w_sem.at[9]),
+        local(wv_hbm, wv, w_sem.at[10]),
     ]
-    wo_copy = local(wo_hbm, wo, w_sem.at[10])
-    part_copy = local(part_scr, part_hbm, w_sem.at[11])
+    wo_copy = local(wo_hbm, wo, w_sem.at[11])
+    part_copy = local(part_scr, part_hbm, w_sem.at[12])
+    gain_rows = g_ref.shape[0]
+    gain_copies = [local(gm_hbm, part_scr.at[8, 0:gain_rows, 0:128], w_sem.at[13]), local(gf_hbm, part_scr.at[8, 32:32 + gain_rows, 0:128], w_sem.at[14])]
     for copy in small + proj_copies:
         copy.start()
 
@@ -68,7 +70,7 @@
         rng = pl.ds(g * GROUP_ROWS, GROUP_ROWS)
         return local(kbuf.at[rng], ko_hbm.at[rng], out_sem.at[0, g]), local(vbuf.at[rng], vo_hbm.at[rng], out_sem.at[1, g])
 
-    for g in range(EARLY_GROUPS):
+    for g in range(groups):
         for copy in loads(g):
             copy.start()
     for copy in small:
@@ -84,18 +86,19 @@
         return vals * cos_part + pltpu.roll(vals, head_dim // 2, 1) * sin_part
 
     q_scr[...] = jnp.zeros_like(q_scr)
-    rms_scaled(normed, 0, x_ref, g_ref)
+    rms_scaled(normed, 0, [x_ref[...]], g_ref)
     for copy in proj_copies:
         copy.wait()
-    for g in range(EARLY_GROUPS, groups):
-        for copy in loads(g):
-            copy.start()
     wo_copy.start()
-    proj = dot(normed[...], w_all[...])
+    for copy in gain_copies:
+        copy.start()
+    q_proj = dot(normed[...], wq[...])
+    k_proj = dot(normed[...], wk[...])
+    v_proj = dot(normed[...], wv[...])
     for h in range(heads):
-        q_scr[pl.ds(h, rows, stride=8), :] = rotate(proj[:, h * head_dim:(h + 1) * head_dim] + bq_ref[h:h + 1, :].astype(F32))
-    kn_scr[...] = rotate(proj[:, q_cols:q_cols + head_dim] + bk_ref[...].astype(F32))
-    vn_scr[...] = proj[:, q_cols + head_dim:q_cols + 2 * head_dim] + bv_ref[...].astype(F32)
+        q_scr[pl.ds(h, rows, stride=8), :] = rotate(q_proj[:, h * head_dim:(h + 1) * head_dim] + bq_ref[h:h + 1, :].astype(F32))
+    kn_scr[...] = rotate(k_proj + bk_ref[...].astype(F32))
+    vn_scr[...] = v_proj + bv_ref[...].astype(F32)
 
     tile_ids = lax.broadcasted_iota(jnp.int32, (16, head_dim), 0)
     slot_ids = lax.broadcasted_iota(jnp.int32, (8, cache_len), 1)
@@ -132,8 +135,15 @@
     attn = jnp.concatenate([o_scr[pl.ds(h, rows, stride=8), :].astype(BF16) for h in range(heads)], axis=1)
     wo_copy.wait()
     part = part_scr.shape[2]
-    for d in range(part_scr.shape[0]):
+    for d in range(8):
         part_scr[d] = dot(attn, wo[:, d * part:(d + 1) * part]).astype(BF16)
+    for copy in gain_copies:
+        copy.wait()
+    for r in range(rows):
+        len_col[r:r + 1, :] = jnp.full((1, head_dim), tok_ref[r], jnp.int32).astype(F32)
+    tok = len_col[...].astype(jnp.int32)
+    digits = jnp.where(lane == 0, tok // 4096, jnp.where(lane == 1, (tok // 64) % 64, tok % 64))
+    part_scr[8, :, 128:256] = digits.astype(F32).astype(BF16)
     part_copy.start()
     for g in range(groups):
         for copy in stores(g):
@@ -141,9 +151,9 @@
     part_copy.wait()
 
 
-def tail_kernel(tok_hbm, gm_hbm, gf_hbm, part_hbm, x_hbm, wg_hbm, wu_hbm, wd_hbm, wh_hbm,
+def tail_kernel(part_hbm, x_hbm, wg_hbm, wu_hbm, wd_hbm, wh_hbm,
                 y_ref, stat_ref,
-                tok_ref, gm_ref, gf_ref, part_ref, x_ref, wg, wu, ring, tok_col,
+                part_ref, x_ref, wg, wu, ring, tok_col,
                 down_ref, half_recv, chip_send, chip_recv, a_full, y_full, normed, gate_act, logits_a, logits_b, run_max, run_sum, run_tgt, stat_send, stat_recv,
                 w_sem, ring_sem, send_sem, recv_sem):
     rows, part = x_ref.shape
@@ -184,9 +194,11 @@
         return copy
 
     small = [local(src, dst, w_sem.at[i]) for i, (src, dst) in enumerate((
-        (part_hbm, part_ref), (x_hbm.at[:, columns(me)], x_ref), (tok_hbm, tok_ref), (gm_hbm, gm_ref), (gf_hbm, gf_ref)))]
-    wg_copy = local(wg_hbm, wg, w_sem.at[5])
-    wu_copy = local(wu_hbm, wu, w_sem.at[6])
+        (part_hbm, part_ref), (x_hbm.at[:, columns(me)], x_ref)))]
+    gain_rows = width // 128
+    gm_ref, gf_ref = part_ref.at[8, 0:gain_rows, 0:128], part_ref.at[8, 32:32 + gain_rows, 0:128]
+    wg_copy = local(wg_hbm, wg, w_sem.at[2])
+    wu_copy = local(wu_hbm, wu, w_sem.at[3])
     wd_copies = [local(wd_hbm.at[pl.ds(i * HEAD_ROWS, HEAD_ROWS)], ring.at[spare + i], ring_sem.at[spare + i]) for i in range(ff // HEAD_ROWS)]
     for copy in small:
         copy.start()
@@ -205,8 +217,9 @@
 
     for copy in small:
         copy.wait()
-    for r in range(rows):
-        tok_col[0, r:r + 1, :] = jnp.full((1, 128), tok_ref[r], jnp.int32)
+    digits = part_ref[8, :, 128:256].astype(F32)
+    tok = digits[:, 0:1] * 4096.0 + digits[:, 1:2] * 64.0 + digits[:, 2:3]
+    tok_col[0] = jnp.broadcast_to(tok, (rows, 128)).astype(jnp.int32)
     pl.semaphore_wait(barrier, len(others))
     push(tok_col.at[0], tok_col.at[1], 4, 15, {'dp': 1 - plane})
 
@@ -216,6 +229,7 @@
         halves = []
         for i, (fy, fx, _) in enumerate(CHIPS + (OWN,)):
             source(peer((fy, fx, 1)), i, True)
+        for i, (fy, fx, _) in enumerate(CHIPS + (OWN,)):
             src = part_ref.at[peer((fy, fx, 1))] if stage == 0 else down_ref.at[i]
             halves.append(push(src, half_recv.at[stage // 2, i], stage, i, sibling))
         mine = [source(peer(flip), i, False) for i, flip in enumerate(CHIPS + (OWN,))]
@@ -233,7 +247,7 @@
 
     def gather(stage, full, planes):
         def block(p, flip):
-            return full.at[p, :, columns(peer(flip))]
+            return full.at[p, peer(flip)]
 
         def move(p, flip, slot, device):
             push(block(p, flip), block(p, flip), stage, slot, device)
@@ -266,13 +280,13 @@
     def attn_source(who, i, send):
         return None if send else part_ref[who].astype(F32)
 
-    a_full[0, :, columns(me)] = scatter_sum(0, attn_source, x_ref[...].astype(F32))
+    a_full[0, me] = scatter_sum(0, attn_source, x_ref[...].astype(F32))
     for copy in wd_copies:
         copy.start()
     gather(1, a_full, 1)
     for i in range(3):
         head_copy(i).start()
-    rms_scaled(normed, 0, a_full.at[0], gm_ref)
+    rms_scaled(normed, 0, [a_full[0, d] for d in range(8)], gm_ref)
     wg_copy.wait()
     wu_copy.wait()
 
@@ -297,13 +311,14 @@
             down_ref[i] = out.astype(BF16)
         return out
 
-    y_full[0, :, columns(me)] = scatter_sum(2, down_source, a_full[0, :, columns(me)].astype(F32))
+    y_full[0, me] = scatter_sum(2, down_source, a_full[0, me].astype(F32))
     for i in range(spare, HEAD_SLOTS):
         head_copy(i).start()
     gather(3, y_full, 2)
-    y_ref[...] = y_full[0]
+    for d in range(8):
+        y_ref[:, d * part:(d + 1) * part] = y_full[0, d]
     for p in range(2):
-        rms_scaled(normed, p * rows, y_full.at[p], gf_ref)
+        rms_scaled(normed, p * rows, [y_full[p, d] for d in range(8)], gf_ref)
     remote(tok_col.at[0], tok_col.at[1], 4, 15, {'dp': 1 - plane}).wait_recv()
     base = me * vocab + plane * half_vocab
     run_max[...] = jnp.full_like(run_max, -jnp.inf)
@@ -398,42 +413,41 @@
     peers = len(FLIPS)
     attn_part, k_all, v_all = pl.pallas_call(
         attention_kernel,
-        out_shape=(jax.ShapeDtypeStruct((8, rows, part), BF16), jax.ShapeDtypeStruct(flat, BF16), jax.ShapeDtypeStruct(flat, BF16)),
-        in_specs=[hbm] * 13,
+        out_shape=(jax.ShapeDtypeStruct((9, rows, part), BF16), jax.ShapeDtypeStruct(flat, BF16), jax.ShapeDtypeStruct(flat, BF16)),
+        in_specs=[hbm] * 16,
         out_specs=(hbm, hbm, hbm),
         scratch_shapes=[
-            pltpu.SMEM((rows,), jnp.int32), pltpu.VMEM((1, head_dim), F32), pltpu.VMEM((width // 128, 128), BF16),
+            pltpu.SMEM((rows,), jnp.int32), pltpu.SMEM((rows,), jnp.int32), pltpu.VMEM((1, head_dim), F32), pltpu.VMEM((width // 128, 128), BF16),
             pltpu.VMEM((w_q.shape[1] // 128, 128), BF16), pltpu.VMEM((1, 128), BF16), pltpu.VMEM((1, 128), BF16),
-            pltpu.VMEM((rows, width), BF16), pltpu.VMEM((width, w_q.shape[1] + 2 * head_dim), BF16), pltpu.VMEM(w_o.shape, BF16),
+            pltpu.VMEM((rows, width), BF16), pltpu.VMEM(w_q.shape, BF16), pltpu.VMEM(w_k.shape, BF16), pltpu.VMEM(w_v.shape, BF16), pltpu.VMEM(w_o.shape, BF16),
             pltpu.VMEM(flat, BF16), pltpu.VMEM(flat, BF16), pltpu.VMEM((rows, width), BF16),
             pltpu.VMEM((rows * 8, head_dim), F32), pltpu.VMEM((rows, head_dim), F32), pltpu.VMEM((rows, head_dim), F32),
-            pltpu.VMEM((rows * 8, head_dim), F32), pltpu.VMEM((rows, head_dim), F32), pltpu.VMEM((8, rows, part), BF16),
-            pltpu.SemaphoreType.DMA((12,)), pltpu.SemaphoreType.DMA((2, groups)), pltpu.SemaphoreType.DMA((2, groups)),
+            pltpu.VMEM((rows * 8, head_dim), F32), pltpu.VMEM((rows, head_dim), F32), pltpu.VMEM((9, rows, part), BF16),
+            pltpu.SemaphoreType.DMA((15,)), pltpu.SemaphoreType.DMA((2, groups)), pltpu.SemaphoreType.DMA((2, groups)),
         ],
         compiler_params=pltpu.CompilerParams(vmem_limit_bytes=67043328),
         name='attention',
-    )(seq_lens, freq, g_attn.reshape(-1, 128), b_q.reshape(-1, 128), b_k.reshape(-1, 128), b_v.reshape(-1, 128),
+    )(seq_lens, next_tok, freq, g_attn.reshape(-1, 128), g_mlp.reshape(-1, 128), g_final.reshape(-1, 128), b_q.reshape(-1, 128), b_k.reshape(-1, 128), b_v.reshape(-1, 128),
       tok_hidden, w_q, w_k, w_v, k_cache.reshape(flat), v_cache.reshape(flat), w_o)
     y_out, stats = pl.pallas_call(
         tail_kernel,
         out_shape=(jax.ShapeDtypeStruct((rows, width), BF16), jax.ShapeDtypeStruct((8, 128), F32)),
-        in_specs=[hbm] * 9,
+        in_specs=[hbm] * 6,
         out_specs=(vmem, vmem),
         scratch_shapes=[
-            pltpu.SMEM((rows,), jnp.int32), pltpu.VMEM((width // 128, 128), BF16), pltpu.VMEM((width // 128, 128), BF16),
-            pltpu.VMEM((8, rows, part), BF16), pltpu.VMEM((rows, part), BF16), pltpu.VMEM(w_gate.shape, BF16), pltpu.VMEM(w_up.shape, BF16),
+            pltpu.VMEM((9, rows, part), BF16), pltpu.VMEM((rows, part), BF16), pltpu.VMEM(w_gate.shape, BF16), pltpu.VMEM(w_up.shape, BF16),
             pltpu.VMEM((HEAD_SLOTS, HEAD_ROWS, width), BF16), pltpu.VMEM((2, rows, 128), jnp.int32),
             pltpu.VMEM((4, rows, part), BF16), pltpu.VMEM((2, 4, rows, part), BF16), pltpu.VMEM((2, 3, rows, part), BF16), pltpu.VMEM((2, 3, rows, part), BF16),
-            pltpu.VMEM((1, rows, width), BF16), pltpu.VMEM((2, rows, width), BF16), pltpu.VMEM((2 * rows, width), BF16), pltpu.VMEM((rows, w_gate.shape[1]), BF16),
+            pltpu.VMEM((1, 8, rows, part), BF16), pltpu.VMEM((2, 8, rows, part), BF16), pltpu.VMEM((2 * rows, width), BF16), pltpu.VMEM((rows, w_gate.shape[1]), BF16),
             pltpu.VMEM((2 * rows, HEAD_ROWS), F32), pltpu.VMEM((2 * rows, HEAD_ROWS), F32),
             pltpu.VMEM((2 * rows, 128), F32), pltpu.VMEM((2 * rows, 128), F32), pltpu.VMEM((2 * rows, 128), F32),
             pltpu.VMEM((8, 128), F32), pltpu.VMEM((2 * peers + 1, 8, 128), F32),
-            pltpu.SemaphoreType.DMA((7,)), pltpu.SemaphoreType.DMA((HEAD_SLOTS,)),
+            pltpu.SemaphoreType.DMA((4,)), pltpu.SemaphoreType.DMA((HEAD_SLOTS,)),
             pltpu.SemaphoreType.DMA((5, 16)), pltpu.SemaphoreType.DMA((5, 16)),
         ],
-        compiler_params=pltpu.CompilerParams(vmem_limit_bytes=57 * 1024 * 1024, collective_id=0, has_side_effects=True),
+        compiler_params=pltpu.CompilerParams(vmem_limit_bytes=54700 * 1024, collective_id=0, has_side_effects=True),
         name='tail',
-    )(next_tok, g_mlp.reshape(-1, 128), g_final.reshape(-1, 128), attn_part, tok_hidden, w_gate, w_up, w_down, w_head)
+    )(attn_part, tok_hidden, w_gate, w_up, w_down, w_head)
     norm_lse = stats[1, :rows]
     return y_out, k_all.reshape(cache_shape), v_all.reshape(cache_shape), stats[0, :rows] - norm_lse, norm_lse
 

time: 77.8 us -> 73 us (0.938)
  Pallas kernels: 73.9 us -> 70.9 us
  local copies, waits for them, and re-layouts: 1.77 us -> 0.75 us
    pallas_call x1, Pallas kernels: 16.8 us -> 15.1 us  [local_step(): pl.pallas_call(attention_kernel, out_shape=(jax.ShapeDtypeStruct((9, rows...]
    pallas_call x1, Pallas kernels: 57.2 us -> 55.8 us  [local_step(): pl.pallas_call(tail_kernel, out_shape=(jax.ShapeDtypeStruct((rows, width)...]
    unnamed x1, local copies, waits for them, and re-layouts: 1.77 us -> 0.75 us
where the time goes in v4:
time: 73 us; the launch traced here: 72.8 us
  Pallas kernels  70.9 us (97%)
  local copies, waits for them, and re-layouts  0.75 us (1%)
    pallas_call x1, Pallas kernels, local_step(): pl.pallas_call(tail_kernel, out_shape=(jax.ShapeDtypeStruct((rows, width)...  55.8 us
    pallas_call x1, Pallas kernels, local_step(): pl.pallas_call(attention_kernel, out_shape=(jax.ShapeDtypeStruct((9, rows...  15.1 us

profile of v4, /device:TPU:0, one launch (start us, length us, event | category | flops | bytes accessed | tf_op | source)
XLA Modules:
  0.0 72.8 jit_solution(16703370744403536698)
XLA Ops:
  0.6 15.1 %attention.1 = (bf16[9,64,384]{2,1,0:T(8,128)(2,1)}, bf16[64,512,128]{2,1,0:T(8,128)(2,1)}, bf16[64,512,128]{2,1,0:T(8,128)(2,1)}) custom-call(s32[64]{0:T(128)} %len_hbm.1, s32[64]{0:T(128)} %tok_hbm.1, f32[1,128]{1,0:T(1,128)} %constant.2.clone.freq_hbm, bf16[24,128]{1,0:T(8,128)(2,1)} %bitcast.21, bf16[24,128]{1,0:T(8,128)(2,1)} %bitcast.22, ...), custom_call_target="tpu_custom_call" | custom-call | tf_op jit(solution)/shard_map/attention/pallas_call | solution.py:414
  15.7 55.8 %tail.1 = (bf16[64,3072]{1,0:T(8,128)(2,1)S(1)}, f32[8,128]{1,0:T(8,128)S(1)}) custom-call(bf16[9,64,384]{2,1,0:T(8,128)(2,1)} %get-tuple-element.10.part_hbm, bf16[64,3072]{1,0:T(8,128)(2,1)} %x_hbm.3, bf16[3072,1024]{1,0:T(8,128)(2,1)} %wg_hbm.1, bf16[3072,1024]{1,0:T(8,128)(2,1)} %wu_hbm.1, bf16[1024,3072]{1,0:T(8,128)(2,1)} %wd_hbm.1, ...), custom_call_target="tpu_custom_call" | custom-call | tf_op jit(solution)/shard_map/tail/pallas_call | solution.py:432
  71.6 0.5 bitcast_subtract_fusion
  72.1 0.7 %copy.28 = bf16[64,3072]{1,0:T(8,128)(2,1)} copy(bf16[64,3072]{1,0:T(8,128)(2,1)S(1)} %get-tuple-element.27) | data formatting | bytes 786432
